TPU v7x, 512 devices: a whole 4x8x8 slice. The times are simulated.
512 devices in a mesh: frames: 64 (over z, y_hi, core), heads: 8 (over y_lo, x).
Axes of the slice: x: 4, y: 8 (y_hi: 4, y_lo: 2; y = y_hi * 2 + y_lo), z: 8, core: 2. Of those that a mesh axis runs over, the one named last changes fastest.
Arguments:
- queries: bfloat16 [16384, 2048], P('frames', 'heads'), may hold values from -8 to 8
- keys: bfloat16 [16384, 2048], P('frames', 'heads'), may hold values from -8 to 8
- values: bfloat16 [16384, 2048], P('frames', 'heads'), may hold values from -6 to 6
- out_grad: bfloat16 [16384, 2048], P('frames', 'heads'), may hold values from -16 to 16
- out_weight: bfloat16 [2048, 2048], P('heads'), may hold values from -0.125 to 0.125
Outputs:
- mixed: bfloat16 [16384, 2048], P('frames', 'heads')
- query_grad: bfloat16 [16384, 2048], P('frames', 'heads')
- key_grad: bfloat16 [16384, 2048], P('frames', 'heads')
- value_grad: bfloat16 [16384, 2048], P('frames', 'heads')
- weight_grad: bfloat16 [2048, 2048], P('heads', 'frames')
All inputs are finite; a program needn't handle non-finite values.
Results may differ from a plain program's by a relative error of at most 0.014.
Values may be sent and summed in bfloat16 or wider, within the bound.
A program may use at most 64 MiB of HBM per device.

v0:
```python
import jax
import jax.numpy as jnp
from jax import lax
from jax.sharding import PartitionSpec as P

HEAD_DIM = 128
REGIONS = 128
WIN = 8
FR_DEV = 2


def shifted(block, axis, distance):
    devices = range(lax.axis_size(axis))
    route = [(i - distance, i) for i in devices if i - distance in devices]
    return lax.ppermute(block, axis, route)


def copy_for_each(array, axis):
    length = lax.axis_size(axis)
    return lax.all_to_all(
        jnp.broadcast_to(array[None], (length, *array.shape)), axis, 0, 0, tiled=True
    )


def joined_along(parts, dim):
    shape = list(parts.shape[1:])
    shape[dim] *= parts.shape[0]
    return jnp.moveaxis(parts, 0, dim).reshape(shape)


def gathered_copies(array, axis, dim):
    parts = copy_for_each(array, axis)
    return joined_along(parts, dim)


def cut_along(array, dim, length):
    shape = array.shape
    parts = array.reshape(*shape[:dim], length, shape[dim] // length, *shape[dim + 1 :])
    return jnp.moveaxis(parts, dim, 0)


def sum_at_owner(array, axis, dim):
    length = lax.axis_size(axis)
    parts = lax.all_to_all(cut_along(array, dim, length), axis, 0, 0, tiled=True)
    return jnp.sum(parts.astype(jnp.float32), axis=0)


def body(queries, keys, values, out_grad, out_weight):
    rows, width = queries.shape
    heads_here = width // HEAD_DIM
    scale = HEAD_DIM ** (-0.5)
    reach = (WIN + FR_DEV - 1) // FR_DEV
    devices = lax.axis_size("frames")
    place = lax.axis_index("frames")
    total_frames = devices * FR_DEV
    offsets = list(range(-reach, reach + 1))
    key_parts = []
    value_parts = []
    for offset in offsets:
        if offset == 0:
            key_parts.append(keys)
            value_parts.append(values)
        else:
            moved = shifted((keys, values), "frames", -offset)
            key_parts.append(moved[0])
            value_parts.append(moved[1])
    wide_keys = jnp.concatenate(key_parts, axis=0)
    wide_values = jnp.concatenate(value_parts, axis=0)
    extent = wide_keys.shape[0]
    middle = reach * rows
    local_rows = jnp.arange(rows, dtype=jnp.int32) // REGIONS
    query_frame = place * FR_DEV + local_rows
    key_frame = (place - reach) * FR_DEV + jnp.arange(extent, dtype=jnp.int32) // REGIONS
    key_live = (key_frame >= 0) & (key_frame < total_frames)
    near = (jnp.abs(query_frame[:, None] - key_frame[None, :]) <= WIN) & key_live[None, :]
    full_grad = gathered_copies(out_grad, "heads", 1)
    grad_attn = jnp.einsum(
        "td,cd->tc", full_grad, out_weight, preferred_element_type=jnp.float32
    ).astype(jnp.bfloat16)
    attn_heads = []
    query_grads = []
    key_cols = []
    value_cols = []
    maxima = []
    totals = []
    deltas = []
    for head in range(heads_here):
        low = head * HEAD_DIM
        query_head = queries[:, low : low + HEAD_DIM]
        key_head = wide_keys[:, low : low + HEAD_DIM]
        value_head = wide_values[:, low : low + HEAD_DIM]
        grad_head = grad_attn[:, low : low + HEAD_DIM]
        scores = (
            jnp.einsum("qd,kd->qk", query_head, key_head, preferred_element_type=jnp.float32)
            * scale
        )
        scores = jnp.where(near, scores, -jnp.inf)
        top = jnp.max(scores, axis=-1)
        expo = jnp.where(near, jnp.exp(scores - top[:, None]), 0.0)
        total = jnp.sum(expo, axis=-1)
        probs = expo / total[:, None]
        weights = probs.astype(jnp.bfloat16)
        attn_heads.append(
            jnp.einsum("qk,kd->qd", weights, value_head, preferred_element_type=jnp.float32)
        )
        dprob = jnp.einsum("qd,kd->qk", grad_head, value_head, preferred_element_type=jnp.float32)
        delta = jnp.sum(probs * dprob, axis=-1)
        dscore = (probs * (dprob - delta[:, None]) * scale).astype(jnp.bfloat16)
        query_grads.append(
            jnp.einsum("qk,kd->qd", dscore, key_head, preferred_element_type=jnp.float32)
        )
        maxima.append(top)
        totals.append(total)
        deltas.append(delta)
        key_cols.append(
            jnp.einsum("qk,qd->kd", dscore, query_head, preferred_element_type=jnp.float32)
        )
        value_cols.append(
            jnp.einsum("qk,qd->kd", weights, grad_head, preferred_element_type=jnp.float32)
        )
    attn = jnp.concatenate(attn_heads, axis=1).astype(jnp.bfloat16)
    query_grad = jnp.concatenate(query_grads, axis=1).astype(jnp.bfloat16)
    partial_out = jnp.dot(attn, out_weight, preferred_element_type=jnp.float32)
    mixed = sum_at_owner(partial_out.astype(jnp.bfloat16), "heads", 1).astype(jnp.bfloat16)
    partial_weight = jnp.einsum("tc,td->cd", attn, full_grad, preferred_element_type=jnp.float32)
    weight_grad = sum_at_owner(partial_weight.astype(jnp.bfloat16), "frames", 1).astype(
        jnp.bfloat16
    )
    wide_key_grad = jnp.concatenate(key_cols, axis=1)
    wide_value_grad = jnp.concatenate(value_cols, axis=1)
    key_total = wide_key_grad[middle : middle + rows]
    value_total = wide_value_grad[middle : middle + rows]
    for offset in offsets:
        if offset != 0:
            begin = (offset + reach) * rows
            back = (
                shifted(
                    wide_key_grad[begin : begin + rows].astype(jnp.bfloat16), "frames", offset
                ).astype(jnp.float32),
                shifted(
                    wide_value_grad[begin : begin + rows].astype(jnp.bfloat16), "frames", offset
                ).astype(jnp.float32),
            )
            key_total = key_total + back[0]
            value_total = value_total + back[1]
    return (
        mixed,
        query_grad,
        key_total.astype(jnp.bfloat16),
        value_total.astype(jnp.bfloat16),
        weight_grad,
    )


def solution(mesh):
    placed = (
        P("frames", "heads"),
        P("frames", "heads"),
        P("frames", "heads"),
        P("frames", "heads"),
        P("heads", None),
    )
    return jax.shard_map(
        body,
        mesh=mesh,
        in_specs=placed,
        out_specs=(
            P("frames", "heads"),
            P("frames", "heads"),
            P("frames", "heads"),
            P("frames", "heads"),
            P("heads", "frames"),
        ),
        check_vma=False,
    )
```

profile of v0, /device:TPU:256, one launch (start us, length us, event | category | flops | bytes accessed | tf_op | source)
XLA Modules:
  0.0 250.9 jit_solution(14146747886389982464)
XLA Ops:
  0.7 7.9 %collective-permute-start = (bf16[256,256]{1,0:T(8,128)(2,1)}, bf16[256,256]{1,0:T(8,128)(2,1)S(1)}, u32[]{:S(2)}, u32[]{:S(2)}) collective-permute-start(bf16[256,256]{1,0:T(8,128)(2,1)} %param.6), channel_id=1, source_target_pairs={{0,32},{8,40},{16,48},{24,56},{32,64},{40,72},{48,80},{56,88},{64,... | collective-permute-start | bytes 393224 | tf_op jit(solution)/shard_map/ppermute | solution.py:15
  8.5 1.9 collective-permute-start.1
  10.5 2.7 %collective-permute-start.2 = (bf16[256,256]{1,0:T(8,128)(2,1)}, bf16[256,256]{1,0:T(8,128)(2,1)S(1)}, u32[]{:S(2)}, u32[]{:S(2)}) collective-permute-start(bf16[256,256]{1,0:T(8,128)(2,1)} %param.6), channel_id=1, source_target_pairs={{0,16},{8,24},{16,32},{24,40},{32,48},{40,56},{48,64},{56,72},{64,... | collective-permute-start | bytes 393224 | tf_op jit(solution)/shard_map/ppermute | solution.py:15
  13.2 4.5 %collective-permute-start.3 = (bf16[256,256]{1,0:T(8,128)(2,1)}, bf16[256,256]{1,0:T(8,128)(2,1)S(1)}, u32[]{:S(2)}, u32[]{:S(2)}) collective-permute-start(bf16[256,256]{1,0:T(8,128)(2,1)} %param.6), channel_id=1, source_target_pairs={{0,8},{8,16},{16,24},{24,32},{32,40},{40,48},{48,56},{56,64},{64,7... | collective-permute-start | bytes 393224 | tf_op jit(solution)/shard_map/ppermute | solution.py:15
  17.7 5.2 %collective-permute-start.4 = (bf16[256,256]{1,0:T(8,128)(2,1)}, bf16[256,256]{1,0:T(8,128)(2,1)S(1)}, u32[]{:S(2)}, u32[]{:S(2)}) collective-permute-start(bf16[256,256]{1,0:T(8,128)(2,1)} %param.6), channel_id=1, source_target_pairs={{8,0},{16,8},{24,16},{32,24},{40,32},{48,40},{56,48},{64,56},{72,6... | collective-permute-start | bytes 393224 | tf_op jit(solution)/shard_map/ppermute | solution.py:15
  25.0 5.4 %all-to-all-start.1 = ((bf16[8,256,256]{1,2,0:T(8,128)(2,1)}), bf16[8,256,256]{1,2,0:T(8,128)(2,1)S(1)}, u32[]{:S(2)}, u32[]{:S(2)}) async-start(bf16[8,256,256]{1,2,0:T(8,128)(2,1)} %broadcast_in_dim.13), calls=%async_computation.1 | async-start | bytes 2097152 | tf_op jit(solution)/shard_map/all_to_all | solution.py:20
  30.5 3.2 %collective-permute-start.5 = (bf16[256,256]{1,0:T(8,128)(2,1)S(1)}, bf16[256,256]{1,0:T(8,128)(2,1)S(1)}, u32[]{:S(2)}, u32[]{:S(2)}) collective-permute-start(bf16[256,256]{1,0:T(8,128)(2,1)S(1)} %copy-done.20), channel_id=1, source_target_pairs={{16,0},{24,8},{32,16},{40,24},{48,32},{56,40},{64,48},{72,56},{80,... | collective-permute-start | bytes 393224 | tf_op jit(solution)/shard_map/ppermute | solution.py:15
  33.7 4.6 %collective-permute-start.6 = (bf16[256,256]{1,0:T(8,128)(2,1)S(1)}, bf16[256,256]{1,0:T(8,128)(2,1)S(1)}, u32[]{:S(2)}, u32[]{:S(2)}) collective-permute-start(bf16[256,256]{1,0:T(8,128)(2,1)S(1)} %copy-done.20), channel_id=1, source_target_pairs={{24,0},{32,8},{40,16},{48,24},{56,32},{64,40},{72,48},{80,56},{88,... | collective-permute-start | bytes 393224 | tf_op jit(solution)/shard_map/ppermute | solution.py:15
  38.3 3.8 %collective-permute-start.7 = (bf16[256,256]{1,0:T(8,128)(2,1)S(1)}, bf16[256,256]{1,0:T(8,128)(2,1)S(1)}, u32[]{:S(2)}, u32[]{:S(2)}) collective-permute-start(bf16[256,256]{1,0:T(8,128)(2,1)S(1)} %copy-done.20), channel_id=1, source_target_pairs={{32,0},{40,8},{48,16},{56,24},{64,32},{72,40},{80,48},{88,56},{96,... | collective-permute-start | bytes 393224 | tf_op jit(solution)/shard_map/ppermute | solution.py:15
  42.2 5.9 %collective-permute-start.8 = (bf16[256,256]{1,0:T(8,128)(2,1)S(1)}, bf16[256,256]{1,0:T(8,128)(2,1)S(1)}, u32[]{:S(2)}, u32[]{:S(2)}) collective-permute-start(bf16[256,256]{1,0:T(8,128)(2,1)S(1)} %copy-done.21), channel_id=1, source_target_pairs={{0,32},{8,40},{16,48},{24,56},{32,64},{40,72},{48,80},{56,88},{64,... | collective-permute-start | bytes 393224 | tf_op jit(solution)/shard_map/ppermute | solution.py:15
  48.2 1.9 collective-permute-start.9
  50.1 5.1 %collective-permute-start.10 = (bf16[256,256]{1,0:T(8,128)(2,1)S(1)}, bf16[256,256]{1,0:T(8,128)(2,1)S(1)}, u32[]{:S(2)}, u32[]{:S(2)}) collective-permute-start(bf16[256,256]{1,0:T(8,128)(2,1)S(1)} %copy-done.21), channel_id=1, source_target_pairs={{0,16},{8,24},{16,32},{24,40},{32,48},{40,56},{48,64},{56,72},{64,... | collective-permute-start | bytes 393224 | tf_op jit(solution)/shard_map/ppermute | solution.py:15
  55.2 1.9 collective-permute-start.11
  57.2 7.9 %collective-permute-start.12 = (bf16[256,256]{1,0:T(8,128)(2,1)S(1)}, bf16[256,256]{1,0:T(8,128)(2,1)S(1)}, u32[]{:S(2)}, u32[]{:S(2)}) collective-permute-start(bf16[256,256]{1,0:T(8,128)(2,1)S(1)} %copy-done.21), channel_id=1, source_target_pairs={{8,0},{16,8},{24,16},{32,24},{40,32},{48,40},{56,48},{64,56},{72,6... | collective-permute-start | bytes 393224 | tf_op jit(solution)/shard_map/ppermute | solution.py:15
  67.2 1.9 collective-permute-start.13
  69.2 4.7 %collective-permute-start.14 = (bf16[256,256]{1,0:T(8,128)(2,1)S(1)}, bf16[256,256]{1,0:T(8,128)(2,1)S(1)}, u32[]{:S(2)}, u32[]{:S(2)}) collective-permute-start(bf16[256,256]{1,0:T(8,128)(2,1)S(1)} %copy-done.21), channel_id=1, source_target_pairs={{24,0},{32,8},{40,16},{48,24},{56,32},{64,40},{72,48},{80,56},{88,... | collective-permute-start | bytes 393224 | tf_op jit(solution)/shard_map/ppermute | solution.py:15
  74.0 4.7 %collective-permute-start.15 = (bf16[256,256]{1,0:T(8,128)(2,1)S(1)}, bf16[256,256]{1,0:T(8,128)(2,1)S(1)}, u32[]{:S(2)}, u32[]{:S(2)}) collective-permute-start(bf16[256,256]{1,0:T(8,128)(2,1)S(1)} %copy-done.21), channel_id=1, source_target_pairs={{32,0},{40,8},{48,16},{56,24},{64,32},{72,40},{80,48},{88,56},{96,... | collective-permute-start | bytes 393224 | tf_op jit(solution)/shard_map/ppermute | solution.py:15
  79.0 9.3 %collective-permute-done.15 = bf16[256,256]{1,0:T(8,128)(2,1)S(1)} collective-permute-done((bf16[256,256]{1,0:T(8,128)(2,1)S(1)}, bf16[256,256]{1,0:T(8,128)(2,1)S(1)}, u32[]{:S(2)}, u32[]{:S(2)}) %collective-permute-start.15) | collective-permute-done | bytes 131104 | tf_op jit(solution)/shard_map/ppermute | solution.py:15
  88.4 2.1 fusion.8
  95.0 9.5 %all-to-all-start = ((bf16[8,256,256]{2,1,0:T(8,128)(2,1)}), bf16[8,256,256]{2,1,0:T(8,128)(2,1)}, u32[]{:S(2)}, u32[]{:S(2)}) async-start(bf16[8,256,256]{2,1,0:T(8,128)(2,1)} %bitcast.28), calls=%async_computation | async-start | bytes 2097152 | tf_op jit(solution)/shard_map/all_to_all | solution.py:44
  106.5 2.9 %fusion.14 = f32[2304,128]{0,1:T(8,128)} fusion(bf16[256,256]{1,0:T(8,128)(2,1)S(1)} %convolution_convert_fusion.2, f32[256,2304]{0,1:T(8,128)S(1)} %copy-done.2, f32[256]{0:T(256)S(1)} %get-tuple-element.22, f32[256]{0:T(256)S(1)} %get-tuple-element.42, pred[2304]{0:T(1024)(128)(4,1)S(1)} %compare_and_fusion, s32[2304]{0:T(1024)S(1)} %fusion.57, ...), kind=kOutput, calls=%fused_computation.37 | convolution fusion | flops 155713536 | bytes 3622912 | tf_op jit(solution)/shard_map/qk,qd->kd/dot_general | solution.py:119
  109.5 3.0 %fusion.11 = f32[2304,128]{0,1:T(8,128)} fusion(bf16[256,256]{1,0:T(8,128)(2,1)S(1)} %convolution_convert_fusion.2, f32[256,2304]{0,1:T(8,128)S(1)} %copy-done.5, f32[256]{0:T(256)S(1)} %get-tuple-element.23, f32[256]{0:T(256)S(1)} %get-tuple-element.44, pred[2304]{0:T(1024)(128)(4,1)S(1)} %compare_and_fusion, s32[2304]{0:T(1024)S(1)} %fusion.57, ...), kind=kOutput, calls=%fused_computation.34 | convolution fusion | flops 155713536 | bytes 3622912 | tf_op jit(solution)/shard_map/qk,qd->kd/dot_general | solution.py:119
  112.9 2.2 copy.32
  118.1 7.8 %collective-permute-start.24 = (bf16[256,256]{0,1:T(8,128)(2,1)}, bf16[256,256]{0,1:T(8,128)(2,1)}, u32[]{:S(2)}, u32[]{:S(2)}) collective-permute-start(bf16[256,256]{0,1:T(8,128)(2,1)} %get-tuple-element.24), channel_id=1, source_target_pairs={{32,0},{40,8},{48,16},{56,24},{64,32},{72,40},{80,48},{88,56},{96,... | collective-permute-start | bytes 393224 | tf_op jit(solution)/shard_map/ppermute | solution.py:15
  125.9 2.6 %collective-permute-start.26 = (bf16[256,256]{0,1:T(8,128)(2,1)}, bf16[256,256]{0,1:T(8,128)(2,1)}, u32[]{:S(2)}, u32[]{:S(2)}) collective-permute-start(bf16[256,256]{0,1:T(8,128)(2,1)} %get-tuple-element.30), channel_id=1, source_target_pairs={{16,0},{24,8},{32,16},{40,24},{48,32},{56,40},{64,48},{72,56},{80,... | collective-permute-start | bytes 393224 | tf_op jit(solution)/shard_map/ppermute | solution.py:15
  128.5 2.1 collective-permute-start.27
  130.7 3.6 %multiply_reduce_fusion.1 = (f32[256]{0:T(256)S(1)}, f32[256]{0:T(256)S(1)}, f32[256,2304]{0,1:T(8,128)S(1)}) fusion(f32[256]{0:T(256)S(1)} %copy-done.31, f32[256,2304]{0,1:T(8,128)S(1)} %copy-done.3, f32[256]{0:T(256)S(1)} %copy-done.27, pred[2304]{0:T(1024)(128)(4,1)S(1)} %compare_and_fusion, s32[2304]{0:T(1024)S(1)} %fusion.57, s32[256]{0:T(256)S(1)} %copy-done.25, ...), kind=kOutput, calls=%fused_computation.19 | convolution fusion | flops 159251968 | bytes 10115072 | tf_op jit(solution)/shard_map/qd,kd->qk/dot_general | solution.py:106
  134.3 3.5 %multiply_convert_fusion.1 = (bf16[256,2304]{0,1:T(8,128)(2,1)}, bf16[256,2304]{0,1:T(8,128)(2,1)S(1)}) fusion(f32[256,2304]{0,1:T(8,128)S(1)} %get-tuple-element.46, f32[256]{0:T(256)S(1)} %get-tuple-element.20, f32[256]{0:T(256)S(1)} %copy-done.31, f32[256,2304]{0,1:T(8,128)S(1)} %copy-done.3, f32[256]{0:T(256)S(1)} %copy-done.27, ...), kind=kLoop, calls=%fused_computation.18 | loop fusion | flops 10616832 | bytes 11815168 | tf_op jit(solution)/shard_map/convert_element_type | solution.py:108
  139.4 12.7 %all-to-all-start.2 = ((bf16[64,256,32]{1,2,0:T(8,128)(2,1)}), bf16[64,256,32]{1,2,0:T(8,128)(2,1)}, u32[]{:S(2)}, u32[]{:S(2)}) async-start(bf16[64,256,32]{1,2,0:T(8,128)(2,1)} %bitcast.7), calls=%async_computation.2 | async-start | bytes 2097152 | tf_op jit(solution)/shard_map/all_to_all | solution.py:44
  156.0 7.0 %collective-permute-start.25 = (bf16[256,256]{0,1:T(8,128)(2,1)S(1)}, bf16[256,256]{0,1:T(8,128)(2,1)S(1)}, u32[]{:S(2)}, u32[]{:S(2)}) collective-permute-start(bf16[256,256]{0,1:T(8,128)(2,1)S(1)} %copy-done.19), channel_id=1, source_target_pairs={{24,0},{32,8},{40,16},{48,24},{56,32},{64,40},{72,48},{80,56},{88,... | collective-permute-start | bytes 393224 | tf_op jit(solution)/shard_map/ppermute | solution.py:15
  163.0 1.9 collective-permute-start.28
  164.9 2.5 collective-permute-start.29
  168.3 18.1 %collective-permute-done.25 = bf16[256,256]{0,1:T(8,128)(2,1)S(1)} collective-permute-done((bf16[256,256]{0,1:T(8,128)(2,1)S(1)}, bf16[256,256]{0,1:T(8,128)(2,1)S(1)}, u32[]{:S(2)}, u32[]{:S(2)}) %collective-permute-start.25) | collective-permute-done | bytes 131104 | tf_op jit(solution)/shard_map/ppermute | solution.py:15
  186.5 4.1 %collective-permute-start.30 = (bf16[256,256]{0,1:T(8,128)(2,1)}, bf16[256,256]{0,1:T(8,128)(2,1)}, u32[]{:S(2)}, u32[]{:S(2)}) collective-permute-start(bf16[256,256]{0,1:T(8,128)(2,1)} %get-tuple-element.26), channel_id=1, source_target_pairs={{0,24},{8,32},{16,40},{24,48},{32,56},{40,64},{48,72},{56,80},{64,... | collective-permute-start | bytes 393224 | tf_op jit(solution)/shard_map/ppermute | solution.py:15
  190.6 2.2 collective-permute-start.31
  192.8 9.7 %collective-permute-start.16 = (bf16[256,256]{0,1:T(8,128)(2,1)}, bf16[256,256]{0,1:T(8,128)(2,1)}, u32[]{:S(2)}, u32[]{:S(2)}) collective-permute-start(bf16[256,256]{0,1:T(8,128)(2,1)} %get-tuple-element.32), channel_id=1, source_target_pairs={{32,0},{40,8},{48,16},{56,24},{64,32},{72,40},{80,48},{88,56},{96,... | collective-permute-start | bytes 393224 | tf_op jit(solution)/shard_map/ppermute | solution.py:15
  202.5 5.1 %collective-permute-start.17 = (bf16[256,256]{0,1:T(8,128)(2,1)}, bf16[256,256]{0,1:T(8,128)(2,1)}, u32[]{:S(2)}, u32[]{:S(2)}) collective-permute-start(bf16[256,256]{0,1:T(8,128)(2,1)} %get-tuple-element.39), channel_id=1, source_target_pairs={{24,0},{32,8},{40,16},{48,24},{56,32},{64,40},{72,48},{80,56},{88,... | collective-permute-start | bytes 393224 | tf_op jit(solution)/shard_map/ppermute | solution.py:15
  207.6 3.0 %collective-permute-start.18 = (bf16[256,256]{0,1:T(8,128)(2,1)}, bf16[256,256]{0,1:T(8,128)(2,1)}, u32[]{:S(2)}, u32[]{:S(2)}) collective-permute-start(bf16[256,256]{0,1:T(8,128)(2,1)} %get-tuple-element.38), channel_id=1, source_target_pairs={{16,0},{24,8},{32,16},{40,24},{48,32},{56,40},{64,48},{72,56},{80,... | collective-permute-start | bytes 393224 | tf_op jit(solution)/shard_map/ppermute | solution.py:15
  211.9 6.3 %collective-permute-start.19 = (bf16[256,256]{0,1:T(8,128)(2,1)}, bf16[256,256]{0,1:T(8,128)(2,1)}, u32[]{:S(2)}, u32[]{:S(2)}) collective-permute-start(bf16[256,256]{0,1:T(8,128)(2,1)} %get-tuple-element.37), channel_id=1, source_target_pairs={{8,0},{16,8},{24,16},{32,24},{40,32},{48,40},{56,48},{64,56},{72,6... | collective-permute-start | bytes 393224 | tf_op jit(solution)/shard_map/ppermute | solution.py:15
  218.3 1.9 collective-permute-start.20
  220.2 1.9 collective-permute-start.21
  222.2 3.7 %collective-permute-start.22 = (bf16[256,256]{0,1:T(8,128)(2,1)}, bf16[256,256]{0,1:T(8,128)(2,1)}, u32[]{:S(2)}, u32[]{:S(2)}) collective-permute-start(bf16[256,256]{0,1:T(8,128)(2,1)} %get-tuple-element.34), channel_id=1, source_target_pairs={{0,24},{8,32},{16,40},{24,48},{32,56},{40,64},{48,72},{56,80},{64,... | collective-permute-start | bytes 393224 | tf_op jit(solution)/shard_map/ppermute | solution.py:15
  225.8 2.8 %collective-permute-start.23 = (bf16[256,256]{0,1:T(8,128)(2,1)}, bf16[256,256]{0,1:T(8,128)(2,1)}, u32[]{:S(2)}, u32[]{:S(2)}) collective-permute-start(bf16[256,256]{0,1:T(8,128)(2,1)} %get-tuple-element.33), channel_id=1, source_target_pairs={{0,32},{8,40},{16,48},{24,56},{32,64},{40,72},{48,80},{56,88},{64,... | collective-permute-start | bytes 393224 | tf_op jit(solution)/shard_map/ppermute | solution.py:15
  231.3 2.4 collective-permute-done.21
  233.7 4.5 %collective-permute-done.22 = bf16[256,256]{0,1:T(8,128)(2,1)} collective-permute-done((bf16[256,256]{0,1:T(8,128)(2,1)}, bf16[256,256]{0,1:T(8,128)(2,1)}, u32[]{:S(2)}, u32[]{:S(2)}) %collective-permute-start.22) | collective-permute-done | bytes 131104 | tf_op jit(solution)/shard_map/ppermute | solution.py:15
  238.3 6.4 %collective-permute-done.23 = bf16[256,256]{0,1:T(8,128)(2,1)} collective-permute-done((bf16[256,256]{0,1:T(8,128)(2,1)}, bf16[256,256]{0,1:T(8,128)(2,1)}, u32[]{:S(2)}, u32[]{:S(2)}) %collective-permute-start.23) | collective-permute-done | bytes 131104 | tf_op jit(solution)/shard_map/ppermute | solution.py:15
  246.8 2.1 reduce_sum.62
  248.9 2.0 reduce_sum.65
  (144 shorter events, 26.9 us)
Async XLA Ops:
  0.6 92.8 %copy-start = (bf16[256,2048]{1,0:T(8,128)(2,1)S(1)}, bf16[256,2048]{1,0:T(8,128)(2,1)}, u32[]{:S(2)}) copy-start(bf16[256,2048]{1,0:T(8,128)(2,1)} %param.9) | copy-start | bytes 3145732
  0.6 29.8 %copy-start.20 = (bf16[256,256]{1,0:T(8,128)(2,1)S(1)}, bf16[256,256]{1,0:T(8,128)(2,1)}, u32[]{:S(2)}) copy-start(bf16[256,256]{1,0:T(8,128)(2,1)} %param.6) | copy-start | bytes 393220
  0.7 41.5 %copy-start.21 = (bf16[256,256]{1,0:T(8,128)(2,1)S(1)}, bf16[256,256]{1,0:T(8,128)(2,1)}, u32[]{:S(2)}) copy-start(bf16[256,256]{1,0:T(8,128)(2,1)} %param.7) | copy-start | bytes 393220
  0.7 29.8 %collective-permute-start = (bf16[256,256]{1,0:T(8,128)(2,1)}, bf16[256,256]{1,0:T(8,128)(2,1)S(1)}, u32[]{:S(2)}, u32[]{:S(2)}) collective-permute-start(bf16[256,256]{1,0:T(8,128)(2,1)} %param.6), channel_id=1, source_target_pairs={{0,32},{8,40},{16,48},{24,56},{32,64},{40,72},{48,80},{56,88},{64,... | collective-permute-start | bytes 393224 | tf_op jit(solution)/shard_map/ppermute | solution.py:15
  8.5 25.2 %collective-permute-start.1 = (bf16[256,256]{1,0:T(8,128)(2,1)}, bf16[256,256]{1,0:T(8,128)(2,1)S(1)}, u32[]{:S(2)}, u32[]{:S(2)}) collective-permute-start(bf16[256,256]{1,0:T(8,128)(2,1)} %param.6), channel_id=1, source_target_pairs={{0,24},{8,32},{16,40},{24,48},{32,56},{40,64},{48,72},{56,80},{64,... | collective-permute-start | bytes 393224 | tf_op jit(solution)/shard_map/ppermute | solution.py:15
  10.5 27.8 %collective-permute-start.2 = (bf16[256,256]{1,0:T(8,128)(2,1)}, bf16[256,256]{1,0:T(8,128)(2,1)S(1)}, u32[]{:S(2)}, u32[]{:S(2)}) collective-permute-start(bf16[256,256]{1,0:T(8,128)(2,1)} %param.6), channel_id=1, source_target_pairs={{0,16},{8,24},{16,32},{24,40},{32,48},{40,56},{48,64},{56,72},{64,... | collective-permute-start | bytes 393224 | tf_op jit(solution)/shard_map/ppermute | solution.py:15
  13.2 29.0 %collective-permute-start.3 = (bf16[256,256]{1,0:T(8,128)(2,1)}, bf16[256,256]{1,0:T(8,128)(2,1)S(1)}, u32[]{:S(2)}, u32[]{:S(2)}) collective-permute-start(bf16[256,256]{1,0:T(8,128)(2,1)} %param.6), channel_id=1, source_target_pairs={{0,8},{8,16},{16,24},{24,32},{32,40},{40,48},{48,56},{56,64},{64,7... | collective-permute-start | bytes 393224 | tf_op jit(solution)/shard_map/ppermute | solution.py:15
  17.7 30.4 %collective-permute-start.4 = (bf16[256,256]{1,0:T(8,128)(2,1)}, bf16[256,256]{1,0:T(8,128)(2,1)S(1)}, u32[]{:S(2)}, u32[]{:S(2)}) collective-permute-start(bf16[256,256]{1,0:T(8,128)(2,1)} %param.6), channel_id=1, source_target_pairs={{8,0},{16,8},{24,16},{32,24},{40,32},{48,40},{56,48},{64,56},{72,6... | collective-permute-start | bytes 393224 | tf_op jit(solution)/shard_map/ppermute | solution.py:15
  25.0 40.1 %copy-start.15 = (bf16[256,256]{1,0:T(8,128)(2,1)S(1)}, bf16[256,256]{1,0:T(8,128)(2,1)}, u32[]{:S(2)}) copy-start(bf16[256,256]{1,0:T(8,128)(2,1)} %param.5) | copy-start | bytes 393220
  25.0 70.0 %all-to-all-start.1 = ((bf16[8,256,256]{1,2,0:T(8,128)(2,1)}), bf16[8,256,256]{1,2,0:T(8,128)(2,1)S(1)}, u32[]{:S(2)}, u32[]{:S(2)}) async-start(bf16[8,256,256]{1,2,0:T(8,128)(2,1)} %broadcast_in_dim.13), calls=%async_computation.1 | async-start | bytes 2097152 | tf_op jit(solution)/shard_map/all_to_all | solution.py:20
  30.4 79.0 %copy-start.24 = (s32[256]{0:T(256)}, s32[256]{0:T(256)S(1)}, u32[]{:S(2)}) copy-start(s32[256]{0:T(256)S(1)} %fusion.61) | copy-start | bytes 3076
  30.5 19.6 %collective-permute-start.5 = (bf16[256,256]{1,0:T(8,128)(2,1)S(1)}, bf16[256,256]{1,0:T(8,128)(2,1)S(1)}, u32[]{:S(2)}, u32[]{:S(2)}) collective-permute-start(bf16[256,256]{1,0:T(8,128)(2,1)S(1)} %copy-done.20), channel_id=1, source_target_pairs={{16,0},{24,8},{32,16},{40,24},{48,32},{56,40},{64,48},{72,56},{80,... | collective-permute-start | bytes 393224 | tf_op jit(solution)/shard_map/ppermute | solution.py:15
  33.7 21.5 %collective-permute-start.6 = (bf16[256,256]{1,0:T(8,128)(2,1)S(1)}, bf16[256,256]{1,0:T(8,128)(2,1)S(1)}, u32[]{:S(2)}, u32[]{:S(2)}) collective-permute-start(bf16[256,256]{1,0:T(8,128)(2,1)S(1)} %copy-done.20), channel_id=1, source_target_pairs={{24,0},{32,8},{40,16},{48,24},{56,32},{64,40},{72,48},{80,56},{88,... | collective-permute-start | bytes 393224 | tf_op jit(solution)/shard_map/ppermute | solution.py:15
  38.3 18.9 %collective-permute-start.7 = (bf16[256,256]{1,0:T(8,128)(2,1)S(1)}, bf16[256,256]{1,0:T(8,128)(2,1)S(1)}, u32[]{:S(2)}, u32[]{:S(2)}) collective-permute-start(bf16[256,256]{1,0:T(8,128)(2,1)S(1)} %copy-done.20), channel_id=1, source_target_pairs={{32,0},{40,8},{48,16},{56,24},{64,32},{72,40},{80,48},{88,56},{96,... | collective-permute-start | bytes 393224 | tf_op jit(solution)/shard_map/ppermute | solution.py:15
  42.2 25.0 %collective-permute-start.8 = (bf16[256,256]{1,0:T(8,128)(2,1)S(1)}, bf16[256,256]{1,0:T(8,128)(2,1)S(1)}, u32[]{:S(2)}, u32[]{:S(2)}) collective-permute-start(bf16[256,256]{1,0:T(8,128)(2,1)S(1)} %copy-done.21), channel_id=1, source_target_pairs={{0,32},{8,40},{16,48},{24,56},{32,64},{40,72},{48,80},{56,88},{64,... | collective-permute-start | bytes 393224 | tf_op jit(solution)/shard_map/ppermute | solution.py:15
  48.2 21.0 %collective-permute-start.9 = (bf16[256,256]{1,0:T(8,128)(2,1)S(1)}, bf16[256,256]{1,0:T(8,128)(2,1)S(1)}, u32[]{:S(2)}, u32[]{:S(2)}) collective-permute-start(bf16[256,256]{1,0:T(8,128)(2,1)S(1)} %copy-done.21), channel_id=1, source_target_pairs={{0,24},{8,32},{16,40},{24,48},{32,56},{40,64},{48,72},{56,80},{64,... | collective-permute-start | bytes 393224 | tf_op jit(solution)/shard_map/ppermute | solution.py:15
  50.1 23.8 %collective-permute-start.10 = (bf16[256,256]{1,0:T(8,128)(2,1)S(1)}, bf16[256,256]{1,0:T(8,128)(2,1)S(1)}, u32[]{:S(2)}, u32[]{:S(2)}) collective-permute-start(bf16[256,256]{1,0:T(8,128)(2,1)S(1)} %copy-done.21), channel_id=1, source_target_pairs={{0,16},{8,24},{16,32},{24,40},{32,48},{40,56},{48,64},{56,72},{64,... | collective-permute-start | bytes 393224 | tf_op jit(solution)/shard_map/ppermute | solution.py:15
  55.2 23.5 %collective-permute-start.11 = (bf16[256,256]{1,0:T(8,128)(2,1)S(1)}, bf16[256,256]{1,0:T(8,128)(2,1)S(1)}, u32[]{:S(2)}, u32[]{:S(2)}) collective-permute-start(bf16[256,256]{1,0:T(8,128)(2,1)S(1)} %copy-done.21), channel_id=1, source_target_pairs={{0,8},{8,16},{16,24},{24,32},{32,40},{40,48},{48,56},{56,64},{64,7... | collective-permute-start | bytes 393224 | tf_op jit(solution)/shard_map/ppermute | solution.py:15
  57.2 21.6 %collective-permute-start.12 = (bf16[256,256]{1,0:T(8,128)(2,1)S(1)}, bf16[256,256]{1,0:T(8,128)(2,1)S(1)}, u32[]{:S(2)}, u32[]{:S(2)}) collective-permute-start(bf16[256,256]{1,0:T(8,128)(2,1)S(1)} %copy-done.21), channel_id=1, source_target_pairs={{8,0},{16,8},{24,16},{32,24},{40,32},{48,40},{56,48},{64,56},{72,6... | collective-permute-start | bytes 393224 | tf_op jit(solution)/shard_map/ppermute | solution.py:15
  66.2 24.3 %copy-start.1 = (f32[256,2304]{0,1:T(8,128)}, f32[256,2304]{0,1:T(8,128)S(1)}, u32[]{:S(2)}) copy-start(f32[256,2304]{0,1:T(8,128)S(1)} %get-tuple-element.43) | copy-start | bytes 7077892
  66.2 40.2 %copy-start.26 = (f32[256]{0:T(256)}, f32[256]{0:T(256)S(1)}, u32[]{:S(2)}) copy-start(f32[256]{0:T(256)S(1)} %get-tuple-element.42) | copy-start | bytes 3076
  67.2 24.7 %copy-start.4 = (f32[256,2304]{0,1:T(8,128)}, f32[256,2304]{0,1:T(8,128)S(1)}, u32[]{:S(2)}) copy-start(f32[256,2304]{0,1:T(8,128)S(1)} %get-tuple-element.45) | copy-start | bytes 7077892
  67.2 42.2 %copy-start.28 = (f32[256]{0:T(256)}, f32[256]{0:T(256)S(1)}, u32[]{:S(2)}) copy-start(f32[256]{0:T(256)S(1)} %get-tuple-element.44) | copy-start | bytes 3076
  67.2 11.6 %collective-permute-start.13 = (bf16[256,256]{1,0:T(8,128)(2,1)S(1)}, bf16[256,256]{1,0:T(8,128)(2,1)S(1)}, u32[]{:S(2)}, u32[]{:S(2)}) collective-permute-start(bf16[256,256]{1,0:T(8,128)(2,1)S(1)} %copy-done.21), channel_id=1, source_target_pairs={{16,0},{24,8},{32,16},{40,24},{48,32},{56,40},{64,48},{72,56},{80,... | collective-permute-start | bytes 393224 | tf_op jit(solution)/shard_map/ppermute | solution.py:15
  69.2 9.8 %collective-permute-start.14 = (bf16[256,256]{1,0:T(8,128)(2,1)S(1)}, bf16[256,256]{1,0:T(8,128)(2,1)S(1)}, u32[]{:S(2)}, u32[]{:S(2)}) collective-permute-start(bf16[256,256]{1,0:T(8,128)(2,1)S(1)} %copy-done.21), channel_id=1, source_target_pairs={{24,0},{32,8},{40,16},{48,24},{56,32},{64,40},{72,48},{80,56},{88,... | collective-permute-start | bytes 393224 | tf_op jit(solution)/shard_map/ppermute | solution.py:15
  74.0 14.4 %collective-permute-start.15 = (bf16[256,256]{1,0:T(8,128)(2,1)S(1)}, bf16[256,256]{1,0:T(8,128)(2,1)S(1)}, u32[]{:S(2)}, u32[]{:S(2)}) collective-permute-start(bf16[256,256]{1,0:T(8,128)(2,1)S(1)} %copy-done.21), channel_id=1, source_target_pairs={{32,0},{40,8},{48,16},{56,24},{64,32},{72,40},{80,48},{88,56},{96,... | collective-permute-start | bytes 393224 | tf_op jit(solution)/shard_map/ppermute | solution.py:15
  90.5 15.9 %copy-start.30 = (f32[256]{0:T(256)}, f32[256]{0:T(256)S(1)}, u32[]{:S(2)}) copy-start(f32[256]{0:T(256)S(1)} %get-tuple-element.22) | copy-start | bytes 3076
  90.5 19.0 %copy-start.32 = (f32[256]{0:T(256)}, f32[256]{0:T(256)S(1)}, u32[]{:S(2)}) copy-start(f32[256]{0:T(256)S(1)} %get-tuple-element.23) | copy-start | bytes 3076
  95.0 44.4 %all-to-all-start = ((bf16[8,256,256]{2,1,0:T(8,128)(2,1)}), bf16[8,256,256]{2,1,0:T(8,128)(2,1)}, u32[]{:S(2)}, u32[]{:S(2)}) async-start(bf16[8,256,256]{2,1,0:T(8,128)(2,1)} %bitcast.28), calls=%async_computation | async-start | bytes 2097152 | tf_op jit(solution)/shard_map/all_to_all | solution.py:44
  118.1 46.8 %collective-permute-start.24 = (bf16[256,256]{0,1:T(8,128)(2,1)}, bf16[256,256]{0,1:T(8,128)(2,1)}, u32[]{:S(2)}, u32[]{:S(2)}) collective-permute-start(bf16[256,256]{0,1:T(8,128)(2,1)} %get-tuple-element.24), channel_id=1, source_target_pairs={{32,0},{40,8},{48,16},{56,24},{64,32},{72,40},{80,48},{88,56},{96,... | collective-permute-start | bytes 393224 | tf_op jit(solution)/shard_map/ppermute | solution.py:15
  125.9 64.7 %collective-permute-start.26 = (bf16[256,256]{0,1:T(8,128)(2,1)}, bf16[256,256]{0,1:T(8,128)(2,1)}, u32[]{:S(2)}, u32[]{:S(2)}) collective-permute-start(bf16[256,256]{0,1:T(8,128)(2,1)} %get-tuple-element.30), channel_id=1, source_target_pairs={{16,0},{24,8},{32,16},{40,24},{48,32},{56,40},{64,48},{72,56},{80,... | collective-permute-start | bytes 393224 | tf_op jit(solution)/shard_map/ppermute | solution.py:15
  128.5 64.3 %collective-permute-start.27 = (bf16[256,256]{0,1:T(8,128)(2,1)}, bf16[256,256]{0,1:T(8,128)(2,1)}, u32[]{:S(2)}, u32[]{:S(2)}) collective-permute-start(bf16[256,256]{0,1:T(8,128)(2,1)} %get-tuple-element.29), channel_id=1, source_target_pairs={{8,0},{16,8},{24,16},{32,24},{40,32},{48,40},{56,48},{64,56},{72,6... | collective-permute-start | bytes 393224 | tf_op jit(solution)/shard_map/ppermute | solution.py:15
  139.4 109.5 %all-to-all-start.2 = ((bf16[64,256,32]{1,2,0:T(8,128)(2,1)}), bf16[64,256,32]{1,2,0:T(8,128)(2,1)}, u32[]{:S(2)}, u32[]{:S(2)}) async-start(bf16[64,256,32]{1,2,0:T(8,128)(2,1)} %bitcast.7), calls=%async_computation.2 | async-start | bytes 2097152 | tf_op jit(solution)/shard_map/all_to_all | solution.py:44
  155.6 55.1 %copy-start.8 = (bf16[256,2304]{0,1:T(8,128)(2,1)S(1)}, bf16[256,2304]{0,1:T(8,128)(2,1)}, u32[]{:S(2)}) copy-start(bf16[256,2304]{0,1:T(8,128)(2,1)} %copy-done.7) | copy-start | bytes 3538948
  156.0 30.5 %collective-permute-start.25 = (bf16[256,256]{0,1:T(8,128)(2,1)S(1)}, bf16[256,256]{0,1:T(8,128)(2,1)S(1)}, u32[]{:S(2)}, u32[]{:S(2)}) collective-permute-start(bf16[256,256]{0,1:T(8,128)(2,1)S(1)} %copy-done.19), channel_id=1, source_target_pairs={{24,0},{32,8},{40,16},{48,24},{56,32},{64,40},{72,48},{80,56},{88,... | collective-permute-start | bytes 393224 | tf_op jit(solution)/shard_map/ppermute | solution.py:15
  163.0 39.6 %collective-permute-start.28 = (bf16[256,256]{0,1:T(8,128)(2,1)S(1)}, bf16[256,256]{0,1:T(8,128)(2,1)S(1)}, u32[]{:S(2)}, u32[]{:S(2)}) collective-permute-start(bf16[256,256]{0,1:T(8,128)(2,1)S(1)} %copy-done.18), channel_id=1, source_target_pairs={{0,8},{8,16},{16,24},{24,32},{32,40},{40,48},{48,56},{56,64},{64,7... | collective-permute-start | bytes 393224 | tf_op jit(solution)/shard_map/ppermute | solution.py:15
  164.9 42.7 %collective-permute-start.29 = (bf16[256,256]{0,1:T(8,128)(2,1)S(1)}, bf16[256,256]{0,1:T(8,128)(2,1)S(1)}, u32[]{:S(2)}, u32[]{:S(2)}) collective-permute-start(bf16[256,256]{0,1:T(8,128)(2,1)S(1)} %copy-done.17), channel_id=1, source_target_pairs={{0,16},{8,24},{16,32},{24,40},{32,48},{40,56},{48,64},{56,72},{64,... | collective-permute-start | bytes 393224 | tf_op jit(solution)/shard_map/ppermute | solution.py:15
  186.5 24.6 %copy-start.12 = (bf16[256,256]{0,1:T(8,128)(2,1)}, bf16[256,256]{0,1:T(8,128)(2,1)S(1)}, u32[]{:S(2)}) copy-start(bf16[256,256]{0,1:T(8,128)(2,1)S(1)} %collective-permute-done.25) | copy-start | bytes 393220
  186.5 25.4 %collective-permute-start.30 = (bf16[256,256]{0,1:T(8,128)(2,1)}, bf16[256,256]{0,1:T(8,128)(2,1)}, u32[]{:S(2)}, u32[]{:S(2)}) collective-permute-start(bf16[256,256]{0,1:T(8,128)(2,1)} %get-tuple-element.26), channel_id=1, source_target_pairs={{0,24},{8,32},{16,40},{24,48},{32,56},{40,64},{48,72},{56,80},{64,... | collective-permute-start | bytes 393224 | tf_op jit(solution)/shard_map/ppermute | solution.py:15
  190.6 27.6 %collective-permute-start.31 = (bf16[256,256]{0,1:T(8,128)(2,1)}, bf16[256,256]{0,1:T(8,128)(2,1)}, u32[]{:S(2)}, u32[]{:S(2)}) collective-permute-start(bf16[256,256]{0,1:T(8,128)(2,1)} %get-tuple-element.25), channel_id=1, source_target_pairs={{0,32},{8,40},{16,48},{24,56},{32,64},{40,72},{48,80},{56,88},{64,... | collective-permute-start | bytes 393224 | tf_op jit(solution)/shard_map/ppermute | solution.py:15
  192.8 27.4 %collective-permute-start.16 = (bf16[256,256]{0,1:T(8,128)(2,1)}, bf16[256,256]{0,1:T(8,128)(2,1)}, u32[]{:S(2)}, u32[]{:S(2)}) collective-permute-start(bf16[256,256]{0,1:T(8,128)(2,1)} %get-tuple-element.32), channel_id=1, source_target_pairs={{32,0},{40,8},{48,16},{56,24},{64,32},{72,40},{80,48},{88,56},{96,... | collective-permute-start | bytes 393224 | tf_op jit(solution)/shard_map/ppermute | solution.py:15
  202.5 19.6 %collective-permute-start.17 = (bf16[256,256]{0,1:T(8,128)(2,1)}, bf16[256,256]{0,1:T(8,128)(2,1)}, u32[]{:S(2)}, u32[]{:S(2)}) collective-permute-start(bf16[256,256]{0,1:T(8,128)(2,1)} %get-tuple-element.39), channel_id=1, source_target_pairs={{24,0},{32,8},{40,16},{48,24},{56,32},{64,40},{72,48},{80,56},{88,... | collective-permute-start | bytes 393224 | tf_op jit(solution)/shard_map/ppermute | solution.py:15
  207.6 18.2 %collective-permute-start.18 = (bf16[256,256]{0,1:T(8,128)(2,1)}, bf16[256,256]{0,1:T(8,128)(2,1)}, u32[]{:S(2)}, u32[]{:S(2)}) collective-permute-start(bf16[256,256]{0,1:T(8,128)(2,1)} %get-tuple-element.38), channel_id=1, source_target_pairs={{16,0},{24,8},{32,16},{40,24},{48,32},{56,40},{64,48},{72,56},{80,... | collective-permute-start | bytes 393224 | tf_op jit(solution)/shard_map/ppermute | solution.py:15
  211.9 19.0 %collective-permute-start.19 = (bf16[256,256]{0,1:T(8,128)(2,1)}, bf16[256,256]{0,1:T(8,128)(2,1)}, u32[]{:S(2)}, u32[]{:S(2)}) collective-permute-start(bf16[256,256]{0,1:T(8,128)(2,1)} %get-tuple-element.37), channel_id=1, source_target_pairs={{8,0},{16,8},{24,16},{32,24},{40,32},{48,40},{56,48},{64,56},{72,6... | collective-permute-start | bytes 393224 | tf_op jit(solution)/shard_map/ppermute | solution.py:15
  218.3 13.0 %collective-permute-start.20 = (bf16[256,256]{0,1:T(8,128)(2,1)}, bf16[256,256]{0,1:T(8,128)(2,1)}, u32[]{:S(2)}, u32[]{:S(2)}) collective-permute-start(bf16[256,256]{0,1:T(8,128)(2,1)} %get-tuple-element.36), channel_id=1, source_target_pairs={{0,8},{8,16},{16,24},{24,32},{32,40},{40,48},{48,56},{56,64},{64,7... | collective-permute-start | bytes 393224 | tf_op jit(solution)/shard_map/ppermute | solution.py:15
  220.2 13.5 %collective-permute-start.21 = (bf16[256,256]{0,1:T(8,128)(2,1)}, bf16[256,256]{0,1:T(8,128)(2,1)}, u32[]{:S(2)}, u32[]{:S(2)}) collective-permute-start(bf16[256,256]{0,1:T(8,128)(2,1)} %get-tuple-element.35), channel_id=1, source_target_pairs={{0,16},{8,24},{16,32},{24,40},{32,48},{40,56},{48,64},{56,72},{64,... | collective-permute-start | bytes 393224 | tf_op jit(solution)/shard_map/ppermute | solution.py:15
  222.2 16.1 %collective-permute-start.22 = (bf16[256,256]{0,1:T(8,128)(2,1)}, bf16[256,256]{0,1:T(8,128)(2,1)}, u32[]{:S(2)}, u32[]{:S(2)}) collective-permute-start(bf16[256,256]{0,1:T(8,128)(2,1)} %get-tuple-element.34), channel_id=1, source_target_pairs={{0,24},{8,32},{16,40},{24,48},{32,56},{40,64},{48,72},{56,80},{64,... | collective-permute-start | bytes 393224 | tf_op jit(solution)/shard_map/ppermute | solution.py:15
  225.8 18.8 %collective-permute-start.23 = (bf16[256,256]{0,1:T(8,128)(2,1)}, bf16[256,256]{0,1:T(8,128)(2,1)}, u32[]{:S(2)}, u32[]{:S(2)}) collective-permute-start(bf16[256,256]{0,1:T(8,128)(2,1)} %get-tuple-element.33), channel_id=1, source_target_pairs={{0,32},{8,40},{16,48},{24,56},{32,64},{40,72},{48,80},{56,88},{64,... | collective-permute-start | bytes 393224 | tf_op jit(solution)/shard_map/ppermute | solution.py:15
  (21 other events, 163.4 us)
where the time goes:
time: 252 us; the launch traced here: 251 us
  starting transfers between devices  160 us (63%)
  waiting for transfers between devices  41.4 us (16%)
  matrix products  20.3 us (8%)
  other arithmetic  14.6 us (6%)
  local copies, waits for them, and re-layouts  12.7 us (5%)
    ppermute x32, starting transfers between devices, shifted(): return lax.ppermute(block, axis, route)  133 us
    ppermute x32, waiting for transfers between devices, shifted(): return lax.ppermute(block, axis, route)  41.4 us
    all_to_all x2, starting transfers between devices, sum_at_owner(): lax.all_to_all(cut_along(array, dim, length), axis, 0, 0, tiled=True)  22.2 us
    unnamed x88, local copies, waits for them, and re-layouts  6.32 us
    dot_general x2, matrix products, body(): jnp.einsum('qk,qd->kd', weights, grad_head, preferred_element_type=jnp.fl...  5.93 us
    all_to_all x1, starting transfers between devices, copy_for_each(): lax.all_to_all(jnp.broadcast_to(array[None], (length, *array.shape)), axi...  5.39 us
  transfers between devices with their start and end apart: 35, of which 7 were waited for; matrix products, arithmetic and copies ran while one was open for 17% of the time, Pallas kernels for 0%

commit v1 on v0

v1 whole, which is shorter than its diff:
```python
import jax
import jax.numpy as jnp
from jax import lax
from jax.experimental import pallas as pl
from jax.experimental.pallas import tpu as pltpu
from jax.sharding import PartitionSpec as P

MESH = pl.DeviceIdType.MESH
BF = jnp.bfloat16
F32 = jnp.float32

NZ = 8
NY = 4
NX = 4
CHIPS = NZ * NY
HD = 128
HALF = 256
TOK = 512
SCALE = HD ** (-0.5)
LOW = -1e30

K, V, Q, G = range(4)


def nt(a, b):
    return lax.dot_general(a, b, (((1,), (1,)), ((), ())), preferred_element_type=F32)


def nn(a, b):
    return jnp.dot(a, b, preferred_element_type=F32)


def kernel(
    q_hbm, k_hbm, v_hbm, og_hbm, w_hbm,
    mixed_out, dq_out, dk_out, dv_out, dw_out,
    k_in, v_in, q_in, g_in, w_in,
    buf, og_mine, og_pair, stat, scores,
    m_ref, l_ref, acc, attn_pair, attn_t, attn_tok, attn_own,
    dq_acc, dk_acc, dv_acc, stage,
    mix_send, mix_recv, mix_keep, mix_tail, mix_land,
    dw_send, dw_recv, dw_part, dw_land,
    load_sem, send_sem, tree_sem, core_sem, og_sem, ogp_sem, stat_sem,
    mix_sem, dwz_sem, dwy_sem, out_sem,
):
    f = lax.axis_index("frames")
    h = lax.axis_index("heads")
    chip = lax.div(f, 2)
    core = lax.rem(f, 2)
    other = 1 - core
    z = lax.div(chip, NY)
    y = lax.rem(chip, NY)
    ylo = lax.div(h, NX)
    x = lax.rem(h, NX)

    def at(c, k):
        return (c * 2 + k, h)

    def along_x(step):
        return (f, ylo * NX + lax.rem(x + step + NX, NX))

    pair = (f + 1 - 2 * core, h)
    across = (f, (1 - ylo) * NX + x)
    mine = pl.ds(pl.multiple_of(core * HALF, HALF), HALF)
    theirs = pl.ds(pl.multiple_of(other * HALF, HALF), HALF)
    my_head = pl.ds(pl.multiple_of(core * HD, HD), HD)
    their_head = pl.ds(pl.multiple_of(other * HD, HD), HD)

    loads = []
    for i, (src, dst) in enumerate((
        (k_hbm, k_in), (v_hbm, v_in), (og_hbm, og_mine.at[h]), (q_hbm, q_in), (w_hbm, w_in),
    )):
        copy = pltpu.make_async_copy(src, dst, load_sem.at[i])
        copy.start()
        loads.append(copy)

    barrier = pltpu.get_barrier_semaphore()
    peers = [pair, across, along_x(1), along_x(2), along_x(3)]
    for step in (1, CHIPS - 1):
        for k in range(2):
            peers.append(at(lax.rem(chip + step, CHIPS), k))
    for step in (2, CHIPS - 2):
        peers.append(at(lax.rem(chip + step, CHIPS), core))
    for step in range(1, NZ):
        peers.append(at(lax.rem(chip + step * NY, CHIPS), core))
    for step in range(1, NY):
        for k in range(2):
            peers.append(at(z * NY + lax.rem(y + step, NY), k))
    for peer in peers:
        pl.semaphore_signal(barrier, inc=1, device_id=peer, device_id_type=MESH)
    pl.semaphore_wait(barrier, len(peers))

    sent = []

    def when(cond, fn):
        if cond is None:
            fn()
        else:
            pl.when(cond)(fn)

    def send(src, dst, sem, device, cond=None):
        slot = len(sent)

        def make():
            return pltpu.make_async_remote_copy(
                src_ref=src, dst_ref=dst, send_sem=send_sem.at[slot], recv_sem=sem,
                device_id=device, device_id_type=MESH,
            )

        sent.append((make, cond))
        when(cond, lambda: make().start())

    def recv(dst, sem, cond=None):
        when(cond, lambda: pltpu.make_async_remote_copy(
            src_ref=dst, dst_ref=dst, send_sem=send_sem.at[0], recv_sem=sem,
            device_id=pair, device_id_type=MESH,
        ).wait_recv())

    def rows(j):
        return pl.ds(j * HALF, HALF)

    def spread(t, src):
        for step, slot in ((1, 1), (-1, 3)):
            cond = chip < CHIPS - 1 if step > 0 else chip > 0
            for k in range(2):
                send(src.at[:, pl.ds(k * HD, HD)], buf.at[t, slot, mine], tree_sem.at[t, slot, core],
                     at(chip + step, k), cond)

    def chunk(t, slot, j):
        return buf.at[t, slot, rows(j)], tree_sem.at[t, slot, j]

    def arrive(t, slot, j, cond):
        recv(*chunk(t, slot, j), cond)

    def pass_on(t, slot, j, to_slot, step, cond):
        dst, sem = chunk(t, to_slot, j)
        send(buf.at[t, slot, rows(j)], dst, sem, at(chip + step, core), cond)

    has_left, has_right = chip >= 1, chip <= CHIPS - 2
    inner = has_left & has_right

    def relay_near(t):
        arrive(t, 1, 0, has_left)
        pass_on(t, 1, 0, 0, 1, inner)
        arrive(t, 3, 1, has_right)
        pass_on(t, 3, 1, 4, -1, inner)
        arrive(t, 1, 1, has_left)
        pass_on(t, 1, 1, 0, 1, has_left & (chip <= 2))
        arrive(t, 3, 0, has_right)
        pass_on(t, 3, 0, 4, -1, has_right & (chip >= CHIPS - 3))

    def relay_far(t):
        arrive(t, 0, 0, chip >= 2)
        pass_on(t, 0, 0, 4, -NY, chip >= NY)
        arrive(t, 4, 1, chip <= CHIPS - 3)
        pass_on(t, 4, 1, 0, NY, chip <= CHIPS - 1 - NY)

    def relay_last(t):
        arrive(t, 0, 1, chip >= 2)
        arrive(t, 4, 0, chip <= CHIPS - 3)

    def live(slot):
        block = chip + slot - 2
        return (block >= 0) & (block < CHIPS)

    loads[0].wait()
    send(k_in.at[:, their_head], buf.at[K, 2, mine], core_sem.at[K], pair)
    spread(K, k_in)
    loads[2].wait()
    send(og_mine.at[h], og_mine.at[h], og_sem.at[h], across)
    send(og_mine.at[h], og_mine.at[h], og_sem.at[h], along_x(1))
    send(og_mine.at[h], og_mine.at[h], og_sem.at[h], along_x(-1))
    loads[1].wait()
    send(v_in.at[:, their_head], buf.at[V, 2, mine], core_sem.at[V], pair)
    spread(V, v_in)
    loads[3].wait()
    send(q_in.at[:, their_head], buf.at[Q, 2, mine], core_sem.at[Q], pair)
    send(og_mine.at[h], og_pair.at[h], ogp_sem.at[h], pair)
    buf[K, 2, mine] = k_in[:, my_head]
    buf[V, 2, mine] = v_in[:, my_head]
    buf[Q, 2, mine] = q_in[:, my_head]
    m_ref[...] = jnp.full_like(m_ref, LOW)
    l_ref[...] = jnp.zeros_like(l_ref)
    acc[...] = jnp.zeros_like(acc)
    dq_acc[...] = jnp.zeros_like(dq_acc)
    dk_acc[...] = jnp.zeros_like(dk_acc)
    dv_acc[...] = jnp.zeros_like(dv_acc)

    def og_take(b):
        recv(og_mine.at[b], og_sem.at[b])
        send(og_mine.at[b], og_pair.at[b], ogp_sem.at[b], pair)

    def og_on(b, step):
        send(og_mine.at[b], og_mine.at[b], og_sem.at[b], along_x(step))

    def block_of(row, step):
        return row * NX + lax.rem(x + step + NX, NX)

    b = block_of(1 - ylo, 0)
    og_take(b)
    og_on(b, 1)
    og_on(b, -1)

    def near_mask(slot, key_frame, query_frame, shape):
        keys = lax.broadcasted_iota(jnp.int32, shape, 0) // HD + key_frame
        queries = lax.broadcasted_iota(jnp.int32, shape, 1) // HD + query_frame
        gap = (keys - queries) * jnp.where(slot == 0, 1, -1)
        return gap >= 0

    def attend(slot, j, masked):
        idx = slot * 2 + j
        keys = buf[K, slot, pl.ds(pl.multiple_of(j * HALF, HALF), HALF)]
        vals_t = buf[V, slot, pl.ds(pl.multiple_of(j * HALF, HALF), HALF)].T
        for part in range(2):
            lanes = pl.ds(part * HALF, HALF)
            s = nt(keys, buf[Q, 2, lanes]) * SCALE
            if masked:
                s = jnp.where(near_mask(slot, 2 * j, 2 * part, s.shape), s, LOW)
            scores[idx, :, lanes] = s
            old = m_ref[:, lanes]
            new = jnp.maximum(old, jnp.max(s, axis=0, keepdims=True))
            p = jnp.exp(s - new)
            fade = jnp.exp(old - new)
            m_ref[:, lanes] = new
            l_ref[:, lanes] = l_ref[:, lanes] * fade + jnp.sum(p, axis=0, keepdims=True)
            acc[:, lanes] = acc[:, lanes] * fade + nn(vals_t, p.astype(BF))

    def attend_all(pairs, masked):
        def step(i, carry):
            slot, j = pairs(i)
            pl.when(live(slot))(lambda: attend(slot, j, masked))
            return carry
        return step

    recv(buf.at[K, 2, theirs], core_sem.at[K])
    recv(buf.at[V, 2, theirs], core_sem.at[V])
    recv(buf.at[Q, 2, theirs], core_sem.at[Q])
    lax.fori_loop(0, 2, attend_all(lambda i: (2, i), False), 0)

    b = block_of(ylo, -1)
    og_take(b)
    og_on(b, 1)
    b = block_of(1 - ylo, 1)
    og_take(b)
    og_on(b, -1)
    og_take(block_of(ylo, 1))
    og_take(block_of(1 - ylo, -1))

    relay_near(K)
    relay_near(V)
    spread(Q, q_in)

    og_take(block_of(ylo, 2))
    og_take(block_of(1 - ylo, 2))
    loads[4].wait()

    grad = jnp.zeros((HALF, HALF), F32)

    def grad_step(i, total):
        cols = pl.ds(pl.multiple_of(i * HALF, HALF), HALF)
        return total + nt(og_mine[i], w_in[:, cols])

    g_in[...] = lax.fori_loop(0, 8, grad_step, grad).astype(BF)
    buf[G, 2, mine] = g_in[:, my_head]
    send(g_in.at[:, their_head], buf.at[G, 2, mine], core_sem.at[G], pair)

    lax.fori_loop(0, 4, attend_all(lambda i: (1 + 2 * lax.rem(i, 2), lax.div(i, 2)), False), 0)

    relay_far(K)
    relay_far(V)
    relay_near(Q)
    spread(G, g_in)
    lax.fori_loop(0, 2, attend_all(lambda i: (4 * i, i), True), 0)
    relay_last(K)
    relay_last(V)
    lax.fori_loop(0, 2, attend_all(lambda i: (4 * i, 1 - i), True), 0)
    recv(buf.at[G, 2, theirs], core_sem.at[G])

    total = l_ref[...]
    out = acc[...] / total
    lse = m_ref[...] + jnp.log(total)
    g_t = buf[G, 2].astype(F32).T
    delta = jnp.sum(g_t * out, axis=0, keepdims=True)
    for i in range(4):
        stat[2, i:i + 1] = lse[:, i * HD:(i + 1) * HD]
        stat[2, 4 + i:5 + i] = delta[:, i * HD:(i + 1) * HD]
    m_ref[...] = lse
    l_ref[...] = delta
    attn_t[...] = out.astype(BF)
    attn_tok[...] = out.T.astype(BF)
    send(attn_tok.at[theirs], attn_own.at[:, my_head], core_sem.at[4], pair)
    attn_own[:, my_head] = attn_tok[mine]
    for step in (1, -1, 2, -2):
        cond = chip + step < CHIPS if step > 0 else chip + step >= 0
        send(stat.at[2], stat.at[2 - step], stat_sem.at[2 - step], at(chip + step, core), cond)

    for b in range(8):
        recv(og_pair.at[b], ogp_sem.at[b])

    def dw_step(i, carry):
        plane = lax.rem(z + i, NZ)
        part = nn(attn_t[:, mine], og_mine[plane]) + nn(attn_t[:, theirs], og_pair[plane])
        dw_send[i] = part.astype(BF)
        return carry

    lax.fori_loop(0, NZ, dw_step, 0)
    for i in (4, 3, 5, 2, 6, 1, 7):
        send(dw_send.at[i], dw_recv.at[i], dwz_sem.at[i], at(lax.rem(z + i, NZ) * NY + y, core))

    recv(attn_own.at[:, their_head], core_sem.at[4])
    for step in (2, 1, 3, 0):
        def mix_step(i, carry):
            cols = pl.ds(pl.multiple_of((i * NX + lax.rem(x + step, NX)) * HALF, HALF), HALF)
            part = nn(attn_own[...], w_in[:, cols])
            if step:
                mix_send[step - 1, i] = part.astype(BF)
            else:
                mix_keep[i] = part
            return carry
        lax.fori_loop(0, 2, mix_step, 0)
        if step:
            send(mix_send.at[step - 1], mix_recv.at[step - 1], mix_sem.at[step - 1], along_x(step))

    relay_far(Q)
    relay_near(G)

    def query_grad(i, carry):
        slot, j = lax.div(i, 2), lax.rem(i, 2)

        def run():
            at_rows = pl.ds(pl.multiple_of(j * HALF, HALF), HALF)
            keys_t = buf[K, slot, at_rows].T
            vals = buf[V, slot, at_rows]
            for part in range(2):
                lanes = pl.ds(part * HALF, HALF)
                p = jnp.exp(scores[i, :, lanes] - m_ref[:, lanes])
                d = nt(vals, buf[G, 2, lanes])
                ds = (p * (d - l_ref[:, lanes]) * SCALE).astype(BF)
                dq_acc[:, lanes] += nn(keys_t, ds)

        pl.when(live(slot))(run)
        return carry

    lax.fori_loop(0, 10, query_grad, 0)
    stage[0] = dq_acc[...].T.astype(BF)
    send(stage.at[0, theirs], dq_out.at[:, my_head], out_sem.at[0], pair)
    dq_out[:, my_head] = stage[0, mine]

    def collect(slot, j, masked):
        at_rows = pl.ds(pl.multiple_of(j * HALF, HALF), HALF)
        qs = buf[Q, slot, at_rows]
        gs = buf[G, slot, at_rows]

        def row(first):
            return jnp.concatenate(
                [stat[slot, pl.ds(first + 2 * j, 1)], stat[slot, pl.ds(first + 2 * j + 1, 1)]], axis=1)

        lse_row, delta_row = row(0), row(4)
        for part in range(2):
            own = pl.ds(part * HALF, HALF)
            s = nt(buf[K, 2, own], qs) * SCALE
            p = jnp.exp(s - lse_row)
            if masked:
                p = jnp.where(near_mask(4 - slot, 2 * part, 2 * j, p.shape), p, 0.0)
            d = nt(buf[V, 2, own], gs)
            ds = (p * (d - delta_row) * SCALE).astype(BF)
            dv_acc[own] += nn(p.astype(BF), gs)
            dk_acc[own] += nn(ds, qs)

    def collect_all(pairs, masked):
        def step(i, carry):
            slot, j = pairs(i)
            pl.when(live(slot))(lambda: collect(slot, j, masked))
            return carry
        return step

    lax.fori_loop(0, 2, collect_all(lambda i: (2, i), False), 0)
    relay_last(Q)

    for step in (1, 2, 3):
        recv(mix_recv.at[step - 1], mix_sem.at[step - 1])

    def mix_sum(i):
        return mix_keep[i] + sum(mix_recv[s, i].astype(F32) for s in range(3))

    mix_tail[...] = mix_sum(1 - ylo).astype(BF)
    send(mix_tail, mix_land, mix_sem.at[3], across)

    for i in (1, 7, 2, 6, 3, 5, 4):
        recv(dw_recv.at[i], dwz_sem.at[i])
    part = dw_send[0].astype(F32)
    for i in range(1, NZ):
        part = part + dw_recv[i].astype(F32)
    dw_part[...] = part.T.astype(BF)

    def cut(yy, k):
        return pl.ds(pl.multiple_of((yy * 2 + k) * 32, 32), 32)

    for step in range(NY):
        yy = lax.rem(y + step, NY)
        for far in range(2):
            k = core if far == 0 else other
            if step == 0 and far == 0:
                dw_land[0, core] = dw_part[cut(yy, k)]
            else:
                send(dw_part.at[cut(yy, k)], dw_land.at[step, core], dwy_sem.at[step, core],
                     at(z * NY + yy, k))

    for i in range(4):
        slot = (1, 3, 0, 4)[i]
        recv(stat.at[slot], stat_sem.at[slot], live(slot))
    relay_far(G)
    lax.fori_loop(0, 4, collect_all(lambda i: (1 + 2 * lax.rem(i, 2), lax.div(i, 2)), False), 0)
    lax.fori_loop(0, 2, collect_all(lambda i: (4 * i, i), True), 0)
    recv(mix_land, mix_sem.at[3])
    mixed_out[...] = (mix_sum(ylo) + mix_land[...].astype(F32)).astype(BF)
    for step in range(NY):
        for far in range(2):
            k = core if far == 0 else other
            if not (step == 0 and far == 0):
                recv(dw_land.at[step, k], dwy_sem.at[step, k])
    for k in range(2):
        piece = sum(dw_land[s, k].astype(F32) for s in range(NY))
        dw_out[k * HD:(k + 1) * HD] = piece.T.astype(BF)
    relay_last(G)
    lax.fori_loop(0, 2, collect_all(lambda i: (4 * i, 1 - i), True), 0)
    for i, (total_ref, out_ref) in enumerate(((dk_acc, dk_out), (dv_acc, dv_out))):
        stage[1 + i] = total_ref[...].astype(BF)
        send(stage.at[1 + i, theirs], out_ref.at[:, my_head], out_sem.at[1 + i], pair)
        out_ref[:, my_head] = stage[1 + i, mine]
    for i, out_ref in enumerate((dq_out, dk_out, dv_out)):
        recv(out_ref.at[:, their_head], out_sem.at[i])
    for make, cond in sent:
        when(cond, lambda: make().wait_send())


SENDS = 128


def body(queries, keys, values, out_grad, out_weight):
    block = jax.ShapeDtypeStruct((HALF, HALF), BF)
    dma = pltpu.SemaphoreType.DMA
    vmem = pltpu.VMEM
    return pl.pallas_call(
        kernel,
        out_shape=(block, block, block, block, jax.ShapeDtypeStruct((HALF, 32), BF)),
        in_specs=[pl.BlockSpec(memory_space=pltpu.HBM)] * 5,
        out_specs=[pl.BlockSpec(memory_space=pltpu.VMEM)] * 5,
        scratch_shapes=[
            vmem((HALF, HALF), BF),
            vmem((HALF, HALF), BF),
            vmem((HALF, HALF), BF),
            vmem((HALF, HALF), BF),
            vmem((HALF, 2048), BF),
            vmem((4, 5, TOK, HD), BF),
            vmem((8, HALF, HALF), BF),
            vmem((8, HALF, HALF), BF),
            vmem((5, 8, HD), F32),
            vmem((10, HALF, TOK), F32),
            vmem((1, TOK), F32),
            vmem((1, TOK), F32),
            vmem((HD, TOK), F32),
            vmem((8, HD), F32),
            vmem((HD, TOK), BF),
            vmem((TOK, HD), BF),
            vmem((HALF, HALF), BF),
            vmem((HD, TOK), F32),
            vmem((TOK, HD), F32),
            vmem((TOK, HD), F32),
            vmem((3, TOK, HD), BF),
            vmem((3, 2, HALF, HALF), BF),
            vmem((3, 2, HALF, HALF), BF),
            vmem((2, HALF, HALF), F32),
            vmem((HALF, HALF), BF),
            vmem((HALF, HALF), BF),
            vmem((NZ, HD, HALF), BF),
            vmem((NZ, HD, HALF), BF),
            vmem((HALF, HD), BF),
            vmem((NY, 2, 32, HD), BF),
            dma((5,)),
            dma((SENDS,)),
            dma((4, 5, 2)),
            dma((5,)),
            dma((8,)),
            dma((8,)),
            dma((5,)),
            dma((4,)),
            dma((NZ,)),
            dma((NY, 2)),
            dma((3,)),
        ],
        compiler_params=pltpu.CompilerParams(
            collective_id=0, has_side_effects=True, vmem_limit_bytes=60 * 2**20
        ),
    )(queries, keys, values, out_grad, out_weight)


def solution(mesh):
    placed = (
        P("frames", "heads"),
        P("frames", "heads"),
        P("frames", "heads"),
        P("frames", "heads"),
        P("heads", None),
    )
    return jax.shard_map(
        body,
        mesh=mesh,
        in_specs=placed,
        out_specs=(
            P("frames", "heads"),
            P("frames", "heads"),
            P("frames", "heads"),
            P("frames", "heads"),
            P("heads", "frames"),
        ),
        check_vma=False,
    )
```

time: 252 us -> 98.3 us (0.39)
  the two profiles are of different devices: /device:TPU:256 before, /device:TPU:9 now
where the time goes in v1:
time: 98.3 us; the launch traced here: 98.1 us
  Pallas kernels  91.7 us (93%)
  local copies, waits for them, and re-layouts  5.69 us (6%)
    pallas_call x1, Pallas kernels, body(): pl.pallas_call(kernel, out_shape=(block, block, block, block, jax.ShapeDt...  91.7 us
    unnamed x10, local copies, waits for them, and re-layouts  4.16 us

profile of v1, /device:TPU:9, one launch (start us, length us, event | category | flops | bytes accessed | tf_op | source)
XLA Modules:
  0.0 98.1 jit_solution(10833078110681581733)
XLA Ops:
  0.6 91.7 %shard_map.92 = (bf16[256,256]{1,0:T(8,128)(2,1)}, bf16[256,256]{1,0:T(8,128)(2,1)}, bf16[256,256]{1,0:T(8,128)(2,1)}, bf16[256,256]{1,0:T(8,128)(2,1)}, bf16[256,32]{1,0:T(8,128)(2,1)}) custom-call(bf16[256,256]{1,0:T(8,128)(2,1)} %q_hbm.1, bf16[256,256]{1,0:T(8,128)(2,1)} %k_hbm.1, bf16[256,256]{1,0:T(8,128)(2,1)} %v_hbm.1, bf16[256,256]{1,0:T(8,128)(2,1)} %og_hbm.1, ...), custom_call_target="tpu_custom_call" | custom-call | tf_op jit(solution)/shard_map/pallas_call | solution.py:443
  92.4 1.5 %copy.10 = bf16[256,32]{0,1:T(8,128)(2,1)} copy(bf16[256,32]{1,0:T(8,128)(2,1)} %get-tuple-element.9) | data formatting | bytes 32768 | tf_op jit(solution)/shard_map/pallas_call | solution.py:443
  93.9 0.0 copy-start.2
  93.9 1.6 %copy.15 = bf16[256,256]{1,0:T(8,128)(2,1)} copy(bf16[256,256]{1,0:T(8,128)(2,1)} %get-tuple-element.15) | data formatting | bytes 262144
  95.5 0.0 copy-done.2
  95.5 0.0 copy-start.1
  95.5 0.7 copy.16
  96.2 0.3 copy-done.1
  96.5 0.0 copy-start
  96.5 0.7 copy.17
  97.1 0.3 copy-done
  97.4 0.7 copy.18
Async XLA Ops:
  93.9 1.6 %copy-start.2 = (bf16[256,256]{1,0:T(8,128)(2,1)S(1)}, bf16[256,256]{1,0:T(8,128)(2,1)}, u32[]{:S(2)}) copy-start(bf16[256,256]{1,0:T(8,128)(2,1)} %get-tuple-element.16) | copy-start | bytes 393220
  95.5 1.0 copy-start.1
  96.5 1.0 copy-start

commit v2 on v1

--- a/solution.py
+++ b/solution.py
@@ -35,12 +35,12 @@
     mixed_out, dq_out, dk_out, dv_out, dw_out,
     k_in, v_in, q_in, g_in, w_in,
     buf, og_mine, og_pair, stat, scores,
-    m_ref, l_ref, acc, attn_pair, attn_t, attn_tok, attn_own,
+    m_ref, l_ref, acc, attn_t, attn_tok, attn_own,
     dq_acc, dk_acc, dv_acc, stage,
     mix_send, mix_recv, mix_keep, mix_tail, mix_land,
     dw_send, dw_recv, dw_part, dw_land,
     load_sem, send_sem, tree_sem, core_sem, og_sem, ogp_sem, stat_sem,
-    mix_sem, dwz_sem, dwy_sem, out_sem,
+    mix_sem, dwz_sem, dwy_sem, out_sem, plane_sem,
 ):
     f = lax.axis_index("frames")
     h = lax.axis_index("heads")
@@ -67,27 +67,55 @@
 
     loads = []
     for i, (src, dst) in enumerate((
-        (k_hbm, k_in), (v_hbm, v_in), (og_hbm, og_mine.at[h]), (q_hbm, q_in), (w_hbm, w_in),
+        (og_hbm, og_mine.at[h]), (k_hbm, k_in), (v_hbm, v_in), (q_hbm, q_in), (w_hbm, w_in),
     )):
         copy = pltpu.make_async_copy(src, dst, load_sem.at[i])
         copy.start()
         loads.append(copy)
 
     barrier = pltpu.get_barrier_semaphore()
+
+    def in_reach(step):
+        return (chip + step >= 0) & (chip + step < CHIPS)
+
+    def greet(device):
+        pl.semaphore_signal(barrier, inc=1, device_id=device, device_id_type=MESH)
+
     peers = [pair, across, along_x(1), along_x(2), along_x(3)]
-    for step in (1, CHIPS - 1):
-        for k in range(2):
-            peers.append(at(lax.rem(chip + step, CHIPS), k))
-    for step in (2, CHIPS - 2):
-        peers.append(at(lax.rem(chip + step, CHIPS), core))
-    for step in range(1, NZ):
-        peers.append(at(lax.rem(chip + step * NY, CHIPS), core))
     for step in range(1, NY):
         for k in range(2):
             peers.append(at(z * NY + lax.rem(y + step, NY), k))
     for peer in peers:
-        pl.semaphore_signal(barrier, inc=1, device_id=peer, device_id_type=MESH)
-    pl.semaphore_wait(barrier, len(peers))
+        greet(peer)
+    expected = len(peers)
+    for step in (1, -1, 2, -2, NY, -NY):
+        def greet_chip(step=step):
+            for k in (0, 1) if abs(step) == 1 else (core,):
+                greet(at(chip + step, k))
+
+        pl.when(in_reach(step))(greet_chip)
+        expected = expected + jnp.where(in_reach(step), 2 if abs(step) == 1 else 1, 0)
+    pl.semaphore_wait(barrier, expected)
+
+    def tell(way, step, cond):
+        pl.when(cond)(lambda: pl.semaphore_signal(
+            plane_sem.at[way], inc=1, device_id=at(chip + step, core), device_id_type=MESH))
+
+    tell(0, NY, z == 0)
+    tell(1, -NY, z == NZ - 1)
+
+    def hear_planes(i):
+        @pl.when(z == i + 1)
+        def _():
+            pl.semaphore_wait(plane_sem.at[0], 1)
+
+        tell(0, NY, (z == i + 1) & (z < NZ - 1))
+
+        @pl.when(z == NZ - 2 - i)
+        def _():
+            pl.semaphore_wait(plane_sem.at[1], 1)
+
+        tell(1, -NY, (z == NZ - 2 - i) & (z > 0))
 
     sent = []
 
@@ -163,17 +191,17 @@
         return (block >= 0) & (block < CHIPS)
 
     loads[0].wait()
-    send(k_in.at[:, their_head], buf.at[K, 2, mine], core_sem.at[K], pair)
-    spread(K, k_in)
-    loads[2].wait()
     send(og_mine.at[h], og_mine.at[h], og_sem.at[h], across)
     send(og_mine.at[h], og_mine.at[h], og_sem.at[h], along_x(1))
     send(og_mine.at[h], og_mine.at[h], og_sem.at[h], along_x(-1))
     loads[1].wait()
+    send(k_in.at[:, their_head], buf.at[K, 2, mine], core_sem.at[K], pair)
+    spread(K, k_in)
+    loads[2].wait()
     send(v_in.at[:, their_head], buf.at[V, 2, mine], core_sem.at[V], pair)
-    spread(V, v_in)
     loads[3].wait()
     send(q_in.at[:, their_head], buf.at[Q, 2, mine], core_sem.at[Q], pair)
+    spread(V, v_in)
     send(og_mine.at[h], og_pair.at[h], ogp_sem.at[h], pair)
     buf[K, 2, mine] = k_in[:, my_head]
     buf[V, 2, mine] = v_in[:, my_head]
@@ -194,11 +222,6 @@
 
     def block_of(row, step):
         return row * NX + lax.rem(x + step + NX, NX)
-
-    b = block_of(1 - ylo, 0)
-    og_take(b)
-    og_on(b, 1)
-    og_on(b, -1)
 
     def near_mask(slot, key_frame, query_frame, shape):
         keys = lax.broadcasted_iota(jnp.int32, shape, 0) // HD + key_frame
@@ -236,19 +259,22 @@
     recv(buf.at[Q, 2, theirs], core_sem.at[Q])
     lax.fori_loop(0, 2, attend_all(lambda i: (2, i), False), 0)
 
+    hear_planes(0)
     b = block_of(ylo, -1)
     og_take(b)
     og_on(b, 1)
+    og_take(block_of(ylo, 1))
+    b = block_of(1 - ylo, 0)
+    og_take(b)
+    og_on(b, 1)
+    og_on(b, -1)
+    hear_planes(1)
     b = block_of(1 - ylo, 1)
     og_take(b)
     og_on(b, -1)
-    og_take(block_of(ylo, 1))
     og_take(block_of(1 - ylo, -1))
-
     relay_near(K)
-    relay_near(V)
-    spread(Q, q_in)
-
+    hear_planes(2)
     og_take(block_of(ylo, 2))
     og_take(block_of(1 - ylo, 2))
     loads[4].wait()
@@ -263,12 +289,16 @@
     buf[G, 2, mine] = g_in[:, my_head]
     send(g_in.at[:, their_head], buf.at[G, 2, mine], core_sem.at[G], pair)
 
+    hear_planes(3)
+    relay_near(V)
+    spread(Q, q_in)
+    hear_planes(4)
     lax.fori_loop(0, 4, attend_all(lambda i: (1 + 2 * lax.rem(i, 2), lax.div(i, 2)), False), 0)
-
     relay_far(K)
+    hear_planes(5)
     relay_far(V)
-    relay_near(Q)
     spread(G, g_in)
+    hear_planes(6)
     lax.fori_loop(0, 2, attend_all(lambda i: (4 * i, i), True), 0)
     relay_last(K)
     relay_last(V)
@@ -293,35 +323,37 @@
         cond = chip + step < CHIPS if step > 0 else chip + step >= 0
         send(stat.at[2], stat.at[2 - step], stat_sem.at[2 - step], at(chip + step, core), cond)
 
+    recv(attn_own.at[:, their_head], core_sem.at[4])
+
+    def mix_part(side, step):
+        row = 1 - ylo if side == 0 else ylo
+        cols = pl.ds(pl.multiple_of((row * NX + lax.rem(x + step, NX)) * HALF, HALF), HALF)
+        return nn(attn_own[...], w_in[:, cols])
+
+    for side in range(2):
+        def mix_step(i, carry):
+            mix_send[i, side] = mix_part(side, i + 1).astype(BF)
+            return carry
+
+        lax.fori_loop(0, 3, mix_step, 0)
+        for i in (1, 0, 2):
+            send(mix_send.at[i, side], mix_recv.at[i, side], mix_sem.at[i, side], along_x(i + 1))
+    relay_near(Q)
+
     for b in range(8):
         recv(og_pair.at[b], ogp_sem.at[b])
 
-    def dw_step(i, carry):
-        plane = lax.rem(z + i, NZ)
+    def dw_step(plane, carry):
         part = nn(attn_t[:, mine], og_mine[plane]) + nn(attn_t[:, theirs], og_pair[plane])
-        dw_send[i] = part.astype(BF)
+        dw_send[plane] = part.astype(BF)
         return carry
 
-    lax.fori_loop(0, NZ, dw_step, 0)
-    for i in (4, 3, 5, 2, 6, 1, 7):
-        send(dw_send.at[i], dw_recv.at[i], dwz_sem.at[i], at(lax.rem(z + i, NZ) * NY + y, core))
-
-    recv(attn_own.at[:, their_head], core_sem.at[4])
-    for step in (2, 1, 3, 0):
-        def mix_step(i, carry):
-            cols = pl.ds(pl.multiple_of((i * NX + lax.rem(x + step, NX)) * HALF, HALF), HALF)
-            part = nn(attn_own[...], w_in[:, cols])
-            if step:
-                mix_send[step - 1, i] = part.astype(BF)
-            else:
-                mix_keep[i] = part
-            return carry
-        lax.fori_loop(0, 2, mix_step, 0)
-        if step:
-            send(mix_send.at[step - 1], mix_recv.at[step - 1], mix_sem.at[step - 1], along_x(step))
-
-    relay_far(Q)
-    relay_near(G)
+    for first in (0, 4):
+        lax.fori_loop(first, first + 4, dw_step, 0)
+        for plane in range(first, first + 4):
+            send(dw_send.at[plane], dw_recv.at[z], dwz_sem.at[z], at(plane * NY + y, core), z != plane)
+    mix_keep[0] = mix_part(0, 0)
+    mix_keep[1] = mix_part(1, 0)
 
     def query_grad(i, carry):
         slot, j = lax.div(i, 2), lax.rem(i, 2)
@@ -339,11 +371,6 @@
 
         pl.when(live(slot))(run)
         return carry
-
-    lax.fori_loop(0, 10, query_grad, 0)
-    stage[0] = dq_acc[...].T.astype(BF)
-    send(stage.at[0, theirs], dq_out.at[:, my_head], out_sem.at[0], pair)
-    dq_out[:, my_head] = stage[0, mine]
 
     def collect(slot, j, masked):
         at_rows = pl.ds(pl.multiple_of(j * HALF, HALF), HALF)
@@ -373,23 +400,34 @@
             return carry
         return step
 
+    lax.fori_loop(0, 4, query_grad, 0)
+    relay_near(G)
+    for slot in (1, 3, 0, 4):
+        recv(stat.at[slot], stat_sem.at[slot], live(slot))
+    relay_far(Q)
+    lax.fori_loop(4, 10, query_grad, 0)
+    stage[0] = dq_acc[...].T.astype(BF)
+    send(stage.at[0, theirs], dq_out.at[:, my_head], out_sem.at[0], pair)
+    dq_out[:, my_head] = stage[0, mine]
     lax.fori_loop(0, 2, collect_all(lambda i: (2, i), False), 0)
-    relay_last(Q)
-
-    for step in (1, 2, 3):
-        recv(mix_recv.at[step - 1], mix_sem.at[step - 1])
-
-    def mix_sum(i):
-        return mix_keep[i] + sum(mix_recv[s, i].astype(F32) for s in range(3))
-
-    mix_tail[...] = mix_sum(1 - ylo).astype(BF)
-    send(mix_tail, mix_land, mix_sem.at[3], across)
-
-    for i in (1, 7, 2, 6, 3, 5, 4):
-        recv(dw_recv.at[i], dwz_sem.at[i])
-    part = dw_send[0].astype(F32)
-    for i in range(1, NZ):
-        part = part + dw_recv[i].astype(F32)
+    relay_far(G)
+
+    def mix_sum(side):
+        for i in range(3):
+            recv(mix_recv.at[i, side], mix_sem.at[i, side])
+        return mix_keep[side] + sum(mix_recv[i, side].astype(F32) for i in range(3))
+
+    mix_tail[...] = mix_sum(0).astype(BF)
+    send(mix_tail, mix_land, mix_sem.at[3, 0], across)
+    lax.fori_loop(0, 4, collect_all(lambda i: (1 + 2 * lax.rem(i, 2), lax.div(i, 2)), False), 0)
+    mix_keep[1] = mix_sum(1)
+
+    dw_recv[z] = dw_send[z]
+    for plane in range(NZ):
+        recv(dw_recv.at[plane], dwz_sem.at[plane], z != plane)
+    part = dw_recv[0].astype(F32)
+    for plane in range(1, NZ):
+        part = part + dw_recv[plane].astype(F32)
     dw_part[...] = part.T.astype(BF)
 
     def cut(yy, k):
@@ -405,34 +443,42 @@
                 send(dw_part.at[cut(yy, k)], dw_land.at[step, core], dwy_sem.at[step, core],
                      at(z * NY + yy, k))
 
-    for i in range(4):
-        slot = (1, 3, 0, 4)[i]
-        recv(stat.at[slot], stat_sem.at[slot], live(slot))
-    relay_far(G)
-    lax.fori_loop(0, 4, collect_all(lambda i: (1 + 2 * lax.rem(i, 2), lax.div(i, 2)), False), 0)
+    relay_last(Q)
     lax.fori_loop(0, 2, collect_all(lambda i: (4 * i, i), True), 0)
-    recv(mix_land, mix_sem.at[3])
-    mixed_out[...] = (mix_sum(ylo) + mix_land[...].astype(F32)).astype(BF)
+    relay_last(G)
+    lax.fori_loop(0, 2, collect_all(lambda i: (4 * i, 1 - i), True), 0)
+    for i, (total_ref, out_ref) in enumerate(((dk_acc, dk_out), (dv_acc, dv_out))):
+        stage[1 + i] = total_ref[...].astype(BF)
+        send(stage.at[1 + i, theirs], out_ref.at[:, my_head], out_sem.at[1 + i], pair)
+        out_ref[:, my_head] = stage[1 + i, mine]
+    recv(mix_land, mix_sem.at[3, 0])
+    mixed_out[...] = (mix_keep[1] + mix_land[...].astype(F32)).astype(BF)
     for step in range(NY):
         for far in range(2):
             k = core if far == 0 else other
             if not (step == 0 and far == 0):
                 recv(dw_land.at[step, k], dwy_sem.at[step, k])
     for k in range(2):
-        piece = sum(dw_land[s, k].astype(F32) for s in range(NY))
-        dw_out[k * HD:(k + 1) * HD] = piece.T.astype(BF)
-    relay_last(G)
-    lax.fori_loop(0, 2, collect_all(lambda i: (4 * i, 1 - i), True), 0)
-    for i, (total_ref, out_ref) in enumerate(((dk_acc, dk_out), (dv_acc, dv_out))):
-        stage[1 + i] = total_ref[...].astype(BF)
-        send(stage.at[1 + i, theirs], out_ref.at[:, my_head], out_sem.at[1 + i], pair)
-        out_ref[:, my_head] = stage[1 + i, mine]
+        dw_out[:, k * HD:(k + 1) * HD] = sum(dw_land[s, k].astype(F32) for s in range(NY)).astype(BF)
     for i, out_ref in enumerate((dq_out, dk_out, dv_out)):
         recv(out_ref.at[:, their_head], out_sem.at[i])
     for make, cond in sent:
         when(cond, lambda: make().wait_send())
 
 
+def finish(*refs):
+    ins, outs, held, sem = refs[:5], refs[5:10], refs[10:15], refs[15]
+    first = [pltpu.make_async_copy(a, b, sem.at[0, i]) for i, (a, b) in enumerate(zip(ins, held))]
+    second = [pltpu.make_async_copy(a, b, sem.at[1, i]) for i, (a, b) in enumerate(zip(held, outs))]
+    for copy in first:
+        copy.start()
+    for a, b in zip(first, second):
+        a.wait()
+        b.start()
+    for copy in second:
+        copy.wait()
+
+
 SENDS = 128
 
 
@@ -440,9 +486,9 @@
     block = jax.ShapeDtypeStruct((HALF, HALF), BF)
     dma = pltpu.SemaphoreType.DMA
     vmem = pltpu.VMEM
-    return pl.pallas_call(
+    results = pl.pallas_call(
         kernel,
-        out_shape=(block, block, block, block, jax.ShapeDtypeStruct((HALF, 32), BF)),
+        out_shape=(block, block, block, block, jax.ShapeDtypeStruct((32, HALF), BF)),
         in_specs=[pl.BlockSpec(memory_space=pltpu.HBM)] * 5,
         out_specs=[pl.BlockSpec(memory_space=pltpu.VMEM)] * 5,
         scratch_shapes=[
@@ -459,7 +505,6 @@
             vmem((1, TOK), F32),
             vmem((1, TOK), F32),
             vmem((HD, TOK), F32),
-            vmem((8, HD), F32),
             vmem((HD, TOK), BF),
             vmem((TOK, HD), BF),
             vmem((HALF, HALF), BF),
@@ -483,15 +528,25 @@
             dma((8,)),
             dma((8,)),
             dma((5,)),
-            dma((4,)),
+            dma((4, 2)),
             dma((NZ,)),
             dma((NY, 2)),
             dma((3,)),
+            pltpu.SemaphoreType.REGULAR((2,)),
         ],
         compiler_params=pltpu.CompilerParams(
             collective_id=0, has_side_effects=True, vmem_limit_bytes=60 * 2**20
         ),
     )(queries, keys, values, out_grad, out_weight)
+    shapes = [jax.ShapeDtypeStruct(r.shape, BF) for r in results]
+    *results, dw = pl.pallas_call(
+        finish,
+        out_shape=shapes,
+        in_specs=[pl.BlockSpec(memory_space=pltpu.HBM)] * 5,
+        out_specs=[pl.BlockSpec(memory_space=pltpu.HBM)] * 5,
+        scratch_shapes=[vmem(r.shape, BF) for r in results] + [dma((2, 5))],
+    )(*results)
+    return (*results, dw.T)
 
 
 def solution(mesh):

time: 98.3 us -> 73 us (0.74)
  Pallas kernels: 91.7 us -> 72.2 us
  local copies, waits for them, and re-layouts: 5.69 us -> 0 us
    pallas_call x1, Pallas kernels: 91.7 us -> 70.3 us  [body(): pl.pallas_call(kernel, out_shape=(block, block, block, block, jax.ShapeDt...]
    unnamed x10 -> x0, local copies, waits for them, and re-layouts: 4.16 us -> none
    pallas_call x0 -> x1, Pallas kernels: none -> 1.84 us  [body(): pl.pallas_call(finish, out_shape=shapes, in_specs=[pl.BlockSpec(memory_sp...]
    pallas_call x1 -> x0, local copies, waits for them, and re-layouts: 1.52 us -> none  [body(): pl.pallas_call(kernel, out_shape=(block, block, block, block, jax.ShapeDt...]
where the time goes in v2:
time: 73 us; the launch traced here: 72.8 us
  Pallas kernels  72.2 us (99%)
    pallas_call x1, Pallas kernels, body(): pl.pallas_call(kernel, out_shape=(block, block, block, block, jax.ShapeDt...  70.3 us
    pallas_call x1, Pallas kernels, body(): pl.pallas_call(finish, out_shape=shapes, in_specs=[pl.BlockSpec(memory_sp...  1.84 us

profile of v2, /device:TPU:9, one launch (start us, length us, event | category | flops | bytes accessed | tf_op | source)
XLA Modules:
  0.0 72.8 jit_solution(3881261302655634178)
XLA Ops:
  0.6 70.3 %shard_map.92 = (bf16[256,256]{1,0:T(8,128)(2,1)}, bf16[256,256]{1,0:T(8,128)(2,1)}, bf16[256,256]{1,0:T(8,128)(2,1)}, bf16[256,256]{1,0:T(8,128)(2,1)}, bf16[32,256]{1,0:T(8,128)(2,1)}) custom-call(bf16[256,256]{1,0:T(8,128)(2,1)} %q_hbm.1, bf16[256,256]{1,0:T(8,128)(2,1)} %k_hbm.1, bf16[256,256]{1,0:T(8,128)(2,1)} %v_hbm.1, bf16[256,256]{1,0:T(8,128)(2,1)} %og_hbm.1, ...), custom_call_target="tpu_custom_call" | custom-call | tf_op jit(solution)/shard_map/pallas_call | solution.py:489
  71.0 1.8 %shard_map.93 = (bf16[256,256]{1,0:T(8,128)(2,1)}, bf16[256,256]{1,0:T(8,128)(2,1)}, bf16[256,256]{1,0:T(8,128)(2,1)}, bf16[256,256]{1,0:T(8,128)(2,1)}, bf16[32,256]{1,0:T(8,128)(2,1)}) custom-call(bf16[256,256]{1,0:T(8,128)(2,1)} %get-tuple-element.15.refs_0_, bf16[256,256]{1,0:T(8,128)(2,1)} %get-tuple-element.16.refs_1_, ...), custom_call_target="tpu_custom_call" | custom-call | tf_op jit(solution)/shard_map/pallas_call | solution.py:542

commit v3 on v2

--- a/solution.py
+++ b/solution.py
@@ -20,6 +20,7 @@
 LOW = -1e30
 
 K, V, Q, G = range(4)
+DETOUR = (V,)
 
 
 def nt(a, b):
@@ -38,9 +39,9 @@
     m_ref, l_ref, acc, attn_t, attn_tok, attn_own,
     dq_acc, dk_acc, dv_acc, stage,
     mix_send, mix_recv, mix_keep, mix_tail, mix_land,
-    dw_send, dw_recv, dw_part, dw_land,
+    dw_send, dw_recv, dw_part, dw_land, detour,
     load_sem, send_sem, tree_sem, core_sem, og_sem, ogp_sem, stat_sem,
-    mix_sem, dwz_sem, dwy_sem, out_sem, plane_sem,
+    mix_sem, dwz_sem, dwy_sem, out_sem, detour_sem, plane_sem,
 ):
     f = lax.axis_index("frames")
     h = lax.axis_index("heads")
@@ -152,6 +153,12 @@
             for k in range(2):
                 send(src.at[:, pl.ds(k * HD, HD)], buf.at[t, slot, mine], tree_sem.at[t, slot, core],
                      at(chip + step, k), cond)
+        if t in DETOUR:
+            i = DETOUR.index(t)
+            for end, step, j in ((0, 3, 1), (CHIPS - 1, -3, 0)):
+                for k in range(2):
+                    send(src.at[:, pl.ds(k * HD, HD)], detour.at[i], detour_sem.at[i],
+                         at(chip + step, k), (chip == end) & (core == j))
 
     def chunk(t, slot, j):
         return buf.at[t, slot, rows(j)], tree_sem.at[t, slot, j]
@@ -171,10 +178,30 @@
         pass_on(t, 1, 0, 0, 1, inner)
         arrive(t, 3, 1, has_right)
         pass_on(t, 3, 1, 4, -1, inner)
+        pass_on(t, 1, 0, 4, -3, chip == CHIPS - 1)
+        pass_on(t, 3, 1, 0, 3, chip == 0)
         arrive(t, 1, 1, has_left)
-        pass_on(t, 1, 1, 0, 1, has_left & (chip <= 2))
         arrive(t, 3, 0, has_right)
-        pass_on(t, 3, 0, 4, -1, has_right & (chip >= CHIPS - 3))
+        if t in DETOUR:
+            i = DETOUR.index(t)
+            for middle, step, slot, j in ((3, -1, 0, 1), (CHIPS - 4, 1, 4, 0)):
+                recv(detour.at[i], detour_sem.at[i], chip == middle)
+                dst, sem = chunk(t, slot, j)
+                send(detour.at[i], dst, sem, at(chip + step, core), chip == middle)
+        else:
+            pass_on(t, 1, 1, 0, 1, chip == 1)
+            pass_on(t, 3, 0, 4, -1, chip == CHIPS - 2)
+
+    def relay_both(t):
+        for j in range(2):
+            for slot, to_slot, step, cond, half in ((1, 0, 1, has_left, j), (3, 4, -1, has_right, 1 - j)):
+                arrive(t, slot, half, cond)
+                pass_on(t, slot, half, to_slot, step, inner)
+
+    def relay_end(t):
+        for j in range(2):
+            arrive(t, 0, j, chip >= 2)
+            arrive(t, 4, j, chip <= CHIPS - 3)
 
     def relay_far(t):
         arrive(t, 0, 0, chip >= 2)
@@ -191,7 +218,6 @@
         return (block >= 0) & (block < CHIPS)
 
     loads[0].wait()
-    send(og_mine.at[h], og_mine.at[h], og_sem.at[h], across)
     send(og_mine.at[h], og_mine.at[h], og_sem.at[h], along_x(1))
     send(og_mine.at[h], og_mine.at[h], og_sem.at[h], along_x(-1))
     loads[1].wait()
@@ -202,6 +228,7 @@
     loads[3].wait()
     send(q_in.at[:, their_head], buf.at[Q, 2, mine], core_sem.at[Q], pair)
     spread(V, v_in)
+    send(og_mine.at[h], og_mine.at[h], og_sem.at[h], across)
     send(og_mine.at[h], og_pair.at[h], ogp_sem.at[h], pair)
     buf[K, 2, mine] = k_in[:, my_head]
     buf[V, 2, mine] = v_in[:, my_head]
@@ -264,61 +291,83 @@
     og_take(b)
     og_on(b, 1)
     og_take(block_of(ylo, 1))
+    hear_planes(1)
+    relay_near(K)
+    hear_planes(2)
+    og_take(block_of(ylo, 2))
+    relay_near(V)
+    hear_planes(3)
+    lax.fori_loop(0, 4, attend_all(lambda i: (1 + 2 * lax.rem(i, 2), lax.div(i, 2)), False), 0)
     b = block_of(1 - ylo, 0)
     og_take(b)
     og_on(b, 1)
     og_on(b, -1)
-    hear_planes(1)
+    hear_planes(4)
+    relay_far(K)
+    hear_planes(5)
+    relay_far(V)
+    spread(Q, q_in)
+    hear_planes(6)
+    lax.fori_loop(0, 2, attend_all(lambda i: (4 * i, i), True), 0)
     b = block_of(1 - ylo, 1)
     og_take(b)
     og_on(b, -1)
     og_take(block_of(1 - ylo, -1))
-    relay_near(K)
-    hear_planes(2)
-    og_take(block_of(ylo, 2))
-    og_take(block_of(1 - ylo, 2))
-    loads[4].wait()
-
-    grad = jnp.zeros((HALF, HALF), F32)
-
-    def grad_step(i, total):
-        cols = pl.ds(pl.multiple_of(i * HALF, HALF), HALF)
-        return total + nt(og_mine[i], w_in[:, cols])
-
-    g_in[...] = lax.fori_loop(0, 8, grad_step, grad).astype(BF)
-    buf[G, 2, mine] = g_in[:, my_head]
-    send(g_in.at[:, their_head], buf.at[G, 2, mine], core_sem.at[G], pair)
-
-    hear_planes(3)
-    relay_near(V)
-    spread(Q, q_in)
-    hear_planes(4)
-    lax.fori_loop(0, 4, attend_all(lambda i: (1 + 2 * lax.rem(i, 2), lax.div(i, 2)), False), 0)
-    relay_far(K)
-    hear_planes(5)
-    relay_far(V)
-    spread(G, g_in)
-    hear_planes(6)
-    lax.fori_loop(0, 2, attend_all(lambda i: (4 * i, i), True), 0)
     relay_last(K)
     relay_last(V)
     lax.fori_loop(0, 2, attend_all(lambda i: (4 * i, 1 - i), True), 0)
-    recv(buf.at[G, 2, theirs], core_sem.at[G])
 
     total = l_ref[...]
     out = acc[...] / total
     lse = m_ref[...] + jnp.log(total)
-    g_t = buf[G, 2].astype(F32).T
-    delta = jnp.sum(g_t * out, axis=0, keepdims=True)
-    for i in range(4):
-        stat[2, i:i + 1] = lse[:, i * HD:(i + 1) * HD]
-        stat[2, 4 + i:5 + i] = delta[:, i * HD:(i + 1) * HD]
     m_ref[...] = lse
-    l_ref[...] = delta
+    acc[...] = out
     attn_t[...] = out.astype(BF)
     attn_tok[...] = out.T.astype(BF)
     send(attn_tok.at[theirs], attn_own.at[:, my_head], core_sem.at[4], pair)
     attn_own[:, my_head] = attn_tok[mine]
+
+    def dw_blocks(row):
+        for step in range(NX):
+            b = block_of(row, step)
+            recv(og_pair.at[b], ogp_sem.at[b])
+
+        def dw_step(i, carry):
+            plane = row * NX + i
+            part = nn(attn_t[:, mine], og_mine[plane]) + nn(attn_t[:, theirs], og_pair[plane])
+            dw_send[plane] = part.astype(BF)
+            return carry
+
+        lax.fori_loop(0, NX, dw_step, 0)
+        for i in range(NX):
+            plane = row * NX + i
+            send(dw_send.at[plane], dw_recv.at[z], dwz_sem.at[z], at(plane * NY + y, core), z != plane)
+
+    dw_blocks(ylo)
+    og_take(block_of(1 - ylo, 2))
+    loads[4].wait()
+
+    grad = jnp.zeros((HALF, HALF), F32)
+
+    def grad_step(i, total):
+        cols = pl.ds(pl.multiple_of(i * HALF, HALF), HALF)
+        return total + nt(og_mine[i], w_in[:, cols])
+
+    g_in[...] = lax.fori_loop(0, 8, grad_step, grad).astype(BF)
+    buf[G, 2, mine] = g_in[:, my_head]
+    send(g_in.at[:, their_head], buf.at[G, 2, mine], core_sem.at[G], pair)
+
+    relay_near(Q)
+    spread(G, g_in)
+    dw_blocks(1 - ylo)
+    recv(buf.at[G, 2, theirs], core_sem.at[G])
+
+    delta = jnp.sum(buf[G, 2].astype(F32).T * acc[...], axis=0, keepdims=True)
+    lse = m_ref[...]
+    for i in range(4):
+        stat[2, i:i + 1] = lse[:, i * HD:(i + 1) * HD]
+        stat[2, 4 + i:5 + i] = delta[:, i * HD:(i + 1) * HD]
+    l_ref[...] = delta
     for step in (1, -1, 2, -2):
         cond = chip + step < CHIPS if step > 0 else chip + step >= 0
         send(stat.at[2], stat.at[2 - step], stat_sem.at[2 - step], at(chip + step, core), cond)
@@ -330,7 +379,7 @@
         cols = pl.ds(pl.multiple_of((row * NX + lax.rem(x + step, NX)) * HALF, HALF), HALF)
         return nn(attn_own[...], w_in[:, cols])
 
-    for side in range(2):
+    def mix_out(side):
         def mix_step(i, carry):
             mix_send[i, side] = mix_part(side, i + 1).astype(BF)
             return carry
@@ -338,20 +387,9 @@
         lax.fori_loop(0, 3, mix_step, 0)
         for i in (1, 0, 2):
             send(mix_send.at[i, side], mix_recv.at[i, side], mix_sem.at[i, side], along_x(i + 1))
-    relay_near(Q)
-
-    for b in range(8):
-        recv(og_pair.at[b], ogp_sem.at[b])
-
-    def dw_step(plane, carry):
-        part = nn(attn_t[:, mine], og_mine[plane]) + nn(attn_t[:, theirs], og_pair[plane])
-        dw_send[plane] = part.astype(BF)
-        return carry
-
-    for first in (0, 4):
-        lax.fori_loop(first, first + 4, dw_step, 0)
-        for plane in range(first, first + 4):
-            send(dw_send.at[plane], dw_recv.at[z], dwz_sem.at[z], at(plane * NY + y, core), z != plane)
+
+    mix_out(0)
+    mix_out(1)
     mix_keep[0] = mix_part(0, 0)
     mix_keep[1] = mix_part(1, 0)
 
@@ -400,17 +438,20 @@
             return carry
         return step
 
-    lax.fori_loop(0, 4, query_grad, 0)
-    relay_near(G)
+    def query_some(first, last):
+        lax.fori_loop(first, last, query_grad, 0)
+
+    def collect_some(count, pairs, masked):
+        lax.fori_loop(0, count, collect_all(pairs, masked), 0)
+
+    query_some(0, 4)
+    relay_far(Q)
+    query_some(4, 8)
+    collect_some(2, lambda i: (2, i), False)
+    relay_both(G)
     for slot in (1, 3, 0, 4):
         recv(stat.at[slot], stat_sem.at[slot], live(slot))
-    relay_far(Q)
-    lax.fori_loop(4, 10, query_grad, 0)
-    stage[0] = dq_acc[...].T.astype(BF)
-    send(stage.at[0, theirs], dq_out.at[:, my_head], out_sem.at[0], pair)
-    dq_out[:, my_head] = stage[0, mine]
-    lax.fori_loop(0, 2, collect_all(lambda i: (2, i), False), 0)
-    relay_far(G)
+    collect_some(4, lambda i: (1 + 2 * lax.rem(i, 2), lax.div(i, 2)), False)
 
     def mix_sum(side):
         for i in range(3):
@@ -419,9 +460,10 @@
 
     mix_tail[...] = mix_sum(0).astype(BF)
     send(mix_tail, mix_land, mix_sem.at[3, 0], across)
-    lax.fori_loop(0, 4, collect_all(lambda i: (1 + 2 * lax.rem(i, 2), lax.div(i, 2)), False), 0)
-    mix_keep[1] = mix_sum(1)
-
+    query_some(8, 10)
+    stage[0] = dq_acc[...].T.astype(BF)
+    send(stage.at[0, theirs], dq_out.at[:, my_head], out_sem.at[0], pair)
+    dq_out[:, my_head] = stage[0, mine]
     dw_recv[z] = dw_send[z]
     for plane in range(NZ):
         recv(dw_recv.at[plane], dwz_sem.at[plane], z != plane)
@@ -444,15 +486,16 @@
                      at(z * NY + yy, k))
 
     relay_last(Q)
-    lax.fori_loop(0, 2, collect_all(lambda i: (4 * i, i), True), 0)
-    relay_last(G)
-    lax.fori_loop(0, 2, collect_all(lambda i: (4 * i, 1 - i), True), 0)
+    relay_end(G)
+    collect_some(4, lambda i: (4 * lax.rem(i, 2), lax.div(i, 2)), True)
     for i, (total_ref, out_ref) in enumerate(((dk_acc, dk_out), (dv_acc, dv_out))):
         stage[1 + i] = total_ref[...].astype(BF)
         send(stage.at[1 + i, theirs], out_ref.at[:, my_head], out_sem.at[1 + i], pair)
         out_ref[:, my_head] = stage[1 + i, mine]
+
+    total = mix_sum(1)
     recv(mix_land, mix_sem.at[3, 0])
-    mixed_out[...] = (mix_keep[1] + mix_land[...].astype(F32)).astype(BF)
+    mixed_out[...] = (total + mix_land[...].astype(F32)).astype(BF)
     for step in range(NY):
         for far in range(2):
             k = core if far == 0 else other
@@ -462,33 +505,29 @@
         dw_out[:, k * HD:(k + 1) * HD] = sum(dw_land[s, k].astype(F32) for s in range(NY)).astype(BF)
     for i, out_ref in enumerate((dq_out, dk_out, dv_out)):
         recv(out_ref.at[:, their_head], out_sem.at[i])
+    assert len(sent) <= SENDS
     for make, cond in sent:
         when(cond, lambda: make().wait_send())
 
 
 def finish(*refs):
-    ins, outs, held, sem = refs[:5], refs[5:10], refs[10:15], refs[15]
-    first = [pltpu.make_async_copy(a, b, sem.at[0, i]) for i, (a, b) in enumerate(zip(ins, held))]
-    second = [pltpu.make_async_copy(a, b, sem.at[1, i]) for i, (a, b) in enumerate(zip(held, outs))]
-    for copy in first:
+    ins, outs, sem = refs[:5], refs[5:10], refs[10]
+    copies = [pltpu.make_async_copy(a, b, sem.at[i]) for i, (a, b) in enumerate(zip(ins, outs))]
+    for copy in copies:
         copy.start()
-    for a, b in zip(first, second):
-        a.wait()
-        b.start()
-    for copy in second:
+    for copy in copies:
         copy.wait()
 
 
-SENDS = 128
+SENDS = 136
 
 
 def body(queries, keys, values, out_grad, out_weight):
-    block = jax.ShapeDtypeStruct((HALF, HALF), BF)
     dma = pltpu.SemaphoreType.DMA
     vmem = pltpu.VMEM
     results = pl.pallas_call(
         kernel,
-        out_shape=(block, block, block, block, jax.ShapeDtypeStruct((32, HALF), BF)),
+        out_shape=(*(pltpu.VMEM((HALF, HALF), BF) for _ in range(4)), pltpu.VMEM((32, HALF), BF)),
         in_specs=[pl.BlockSpec(memory_space=pltpu.HBM)] * 5,
         out_specs=[pl.BlockSpec(memory_space=pltpu.VMEM)] * 5,
         scratch_shapes=[
@@ -521,6 +560,7 @@
             vmem((NZ, HD, HALF), BF),
             vmem((HALF, HD), BF),
             vmem((NY, 2, 32, HD), BF),
+            vmem((1, HALF, HD), BF),
             dma((5,)),
             dma((SENDS,)),
             dma((4, 5, 2)),
@@ -532,6 +572,7 @@
             dma((NZ,)),
             dma((NY, 2)),
             dma((3,)),
+            dma((1,)),
             pltpu.SemaphoreType.REGULAR((2,)),
         ],
         compiler_params=pltpu.CompilerParams(
@@ -542,10 +583,10 @@
     *results, dw = pl.pallas_call(
         finish,
         out_shape=shapes,
-        in_specs=[pl.BlockSpec(memory_space=pltpu.HBM)] * 5,
+        in_specs=[pl.BlockSpec(memory_space=pltpu.VMEM)] * 5,
         out_specs=[pl.BlockSpec(memory_space=pltpu.HBM)] * 5,
-        scratch_shapes=[vmem(r.shape, BF) for r in results] + [dma((2, 5))],
-    )(*results)
+        scratch_shapes=[dma((5,))],
+    )(*(pltpu.with_memory_space_constraint(r, pltpu.VMEM) for r in results))
     return (*results, dw.T)
 
 

time: 73 us -> 71.3 us (0.977)
  the two profiles are of different devices: /device:TPU:9 before, /device:TPU:137 now
where the time goes in v3:
time: 71.3 us; the launch traced here: 71.2 us
  Pallas kernels  70.6 us (99%)
    pallas_call x1, Pallas kernels, body(): pl.pallas_call(kernel, out_shape=(*(pltpu.VMEM((HALF, HALF), BF) for _ in...  69.7 us

profile of v3, /device:TPU:137, one launch (start us, length us, event | category | flops | bytes accessed | tf_op | source)
XLA Modules:
  0.0 71.2 jit_solution(414912248333979087)
XLA Ops:
  0.6 69.7 %shard_map.92 = (bf16[256,256]{1,0:T(8,128)(2,1)S(1)}, bf16[256,256]{1,0:T(8,128)(2,1)S(1)}, bf16[256,256]{1,0:T(8,128)(2,1)S(1)}, bf16[256,256]{1,0:T(8,128)(2,1)S(1)}, bf16[32,256]{1,0:T(8,128)(2,1)S(1)}) custom-call(bf16[256,256]{1,0:T(8,128)(2,1)} %q_hbm.1, bf16[256,256]{1,0:T(8,128)(2,1)} %k_hbm.1, bf16[256,256]{1,0:T(8,128)(2,1)} %v_hbm.1, ...), custom_call_target="tpu_custom_call" | custom-call | tf_op jit(solution)/shard_map/pallas_call | solution.py:528
  70.4 0.8 %shard_map.93 = (bf16[256,256]{1,0:T(8,128)(2,1)}, bf16[256,256]{1,0:T(8,128)(2,1)}, bf16[256,256]{1,0:T(8,128)(2,1)}, bf16[256,256]{1,0:T(8,128)(2,1)}, bf16[32,256]{1,0:T(8,128)(2,1)}) custom-call(bf16[256,256]{1,0:T(8,128)(2,1)S(1)} %get-tuple-element.15.refs_0_, bf16[256,256]{1,0:T(8,128)(2,1)S(1)} %get-tuple-element.16.refs_1_, ...), custom_call_target="tpu_custom_call" | custom-call | tf_op jit(solution)/shard_map/pallas_call | solution.py:583

commit v4 on v3

--- a/solution.py
+++ b/solution.py
@@ -304,15 +304,24 @@
     og_on(b, -1)
     hear_planes(4)
     relay_far(K)
-    hear_planes(5)
     relay_far(V)
     spread(Q, q_in)
-    hear_planes(6)
     lax.fori_loop(0, 2, attend_all(lambda i: (4 * i, i), True), 0)
     b = block_of(1 - ylo, 1)
     og_take(b)
     og_on(b, -1)
     og_take(block_of(1 - ylo, -1))
+    hear_planes(5)
+
+    loads[4].wait()
+
+    def grad_part(b):
+        return nt(og_mine[b], w_in[:, pl.ds(pl.multiple_of(b * HALF, HALF), HALF)])
+
+    grad = grad_part(block_of(ylo, 0))
+    for row, step in ((ylo, 1), (ylo, 2), (ylo, 3), (1 - ylo, 0), (1 - ylo, 1), (1 - ylo, 3)):
+        grad = grad + grad_part(block_of(row, step))
+    mix_keep[0] = grad
     relay_last(K)
     relay_last(V)
     lax.fori_loop(0, 2, attend_all(lambda i: (4 * i, 1 - i), True), 0)
@@ -343,23 +352,15 @@
             plane = row * NX + i
             send(dw_send.at[plane], dw_recv.at[z], dwz_sem.at[z], at(plane * NY + y, core), z != plane)
 
-    dw_blocks(ylo)
     og_take(block_of(1 - ylo, 2))
-    loads[4].wait()
-
-    grad = jnp.zeros((HALF, HALF), F32)
-
-    def grad_step(i, total):
-        cols = pl.ds(pl.multiple_of(i * HALF, HALF), HALF)
-        return total + nt(og_mine[i], w_in[:, cols])
-
-    g_in[...] = lax.fori_loop(0, 8, grad_step, grad).astype(BF)
+    g_in[...] = (mix_keep[0] + grad_part(block_of(1 - ylo, 2))).astype(BF)
     buf[G, 2, mine] = g_in[:, my_head]
     send(g_in.at[:, their_head], buf.at[G, 2, mine], core_sem.at[G], pair)
-
+    spread(G, g_in)
+    hear_planes(6)
+    dw_blocks(ylo)
+    dw_blocks(1 - ylo)
     relay_near(Q)
-    spread(G, g_in)
-    dw_blocks(1 - ylo)
     recv(buf.at[G, 2, theirs], core_sem.at[G])
 
     delta = jnp.sum(buf[G, 2].astype(F32).T * acc[...], axis=0, keepdims=True)
@@ -445,10 +446,10 @@
         lax.fori_loop(0, count, collect_all(pairs, masked), 0)
 
     query_some(0, 4)
+    relay_both(G)
+    collect_some(2, lambda i: (2, i), False)
+    query_some(4, 6)
     relay_far(Q)
-    query_some(4, 8)
-    collect_some(2, lambda i: (2, i), False)
-    relay_both(G)
     for slot in (1, 3, 0, 4):
         recv(stat.at[slot], stat_sem.at[slot], live(slot))
     collect_some(4, lambda i: (1 + 2 * lax.rem(i, 2), lax.div(i, 2)), False)
@@ -460,7 +461,7 @@
 
     mix_tail[...] = mix_sum(0).astype(BF)
     send(mix_tail, mix_land, mix_sem.at[3, 0], across)
-    query_some(8, 10)
+    query_some(6, 10)
     stage[0] = dq_acc[...].T.astype(BF)
     send(stage.at[0, theirs], dq_out.at[:, my_head], out_sem.at[0], pair)
     dq_out[:, my_head] = stage[0, mine]

time: 71.3 us -> 71 us (level)
  the two profiles are of different devices: /device:TPU:137 before, /device:TPU:41 now
where the time goes in v4:
time: 71 us; the launch traced here: 70.8 us
  Pallas kernels  70.2 us (99%)
    pallas_call x1, Pallas kernels, body(): pl.pallas_call(kernel, out_shape=(*(pltpu.VMEM((HALF, HALF), BF) for _ in...  69.4 us

profile of v4, /device:TPU:41, one launch (start us, length us, event | category | flops | bytes accessed | tf_op | source)
XLA Modules:
  0.0 70.8 jit_solution(15924381377067511199)
XLA Ops:
  0.6 69.4 %shard_map.92 = (bf16[256,256]{1,0:T(8,128)(2,1)S(1)}, bf16[256,256]{1,0:T(8,128)(2,1)S(1)}, bf16[256,256]{1,0:T(8,128)(2,1)S(1)}, bf16[256,256]{1,0:T(8,128)(2,1)S(1)}, bf16[32,256]{1,0:T(8,128)(2,1)S(1)}) custom-call(bf16[256,256]{1,0:T(8,128)(2,1)} %q_hbm.1, bf16[256,256]{1,0:T(8,128)(2,1)} %k_hbm.1, bf16[256,256]{1,0:T(8,128)(2,1)} %v_hbm.1, ...), custom_call_target="tpu_custom_call" | custom-call | tf_op jit(solution)/shard_map/pallas_call | solution.py:529
  70.0 0.8 %shard_map.93 = (bf16[256,256]{1,0:T(8,128)(2,1)}, bf16[256,256]{1,0:T(8,128)(2,1)}, bf16[256,256]{1,0:T(8,128)(2,1)}, bf16[256,256]{1,0:T(8,128)(2,1)}, bf16[32,256]{1,0:T(8,128)(2,1)}) custom-call(bf16[256,256]{1,0:T(8,128)(2,1)S(1)} %get-tuple-element.15.refs_0_, bf16[256,256]{1,0:T(8,128)(2,1)S(1)} %get-tuple-element.16.refs_1_, ...), custom_call_target="tpu_custom_call" | custom-call | tf_op jit(solution)/shard_map/pallas_call | solution.py:584

commit v5 on v4

--- a/solution.py
+++ b/solution.py
@@ -20,7 +20,7 @@
 LOW = -1e30
 
 K, V, Q, G = range(4)
-DETOUR = (V,)
+DETOUR = (V, Q)
 
 
 def nt(a, b):
@@ -561,7 +561,7 @@
             vmem((NZ, HD, HALF), BF),
             vmem((HALF, HD), BF),
             vmem((NY, 2, 32, HD), BF),
-            vmem((1, HALF, HD), BF),
+            vmem((2, HALF, HD), BF),
             dma((5,)),
             dma((SENDS,)),
             dma((4, 5, 2)),
@@ -573,7 +573,7 @@
             dma((NZ,)),
             dma((NY, 2)),
             dma((3,)),
-            dma((1,)),
+            dma((2,)),
             pltpu.SemaphoreType.REGULAR((2,)),
         ],
         compiler_params=pltpu.CompilerParams(

time: 71 us -> 71 us (level)
  no operation moved by 1% of the time
where the time goes in v5:
time: 71 us; the launch traced here: 70.9 us
  Pallas kernels  70.2 us (99%)
    pallas_call x1, Pallas kernels, body(): pl.pallas_call(kernel, out_shape=(*(pltpu.VMEM((HALF, HALF), BF) for _ in...  69.4 us

profile of v5, /device:TPU:41, one launch (start us, length us, event | category | flops | bytes accessed | tf_op | source)
XLA Modules:
  0.0 70.9 jit_solution(681666679066250308)
XLA Ops:
  0.6 69.4 %shard_map.92 = (bf16[256,256]{1,0:T(8,128)(2,1)S(1)}, bf16[256,256]{1,0:T(8,128)(2,1)S(1)}, bf16[256,256]{1,0:T(8,128)(2,1)S(1)}, bf16[256,256]{1,0:T(8,128)(2,1)S(1)}, bf16[32,256]{1,0:T(8,128)(2,1)S(1)}) custom-call(bf16[256,256]{1,0:T(8,128)(2,1)} %q_hbm.1, bf16[256,256]{1,0:T(8,128)(2,1)} %k_hbm.1, bf16[256,256]{1,0:T(8,128)(2,1)} %v_hbm.1, ...), custom_call_target="tpu_custom_call" | custom-call | tf_op jit(solution)/shard_map/pallas_call | solution.py:529
  70.0 0.8 %shard_map.93 = (bf16[256,256]{1,0:T(8,128)(2,1)}, bf16[256,256]{1,0:T(8,128)(2,1)}, bf16[256,256]{1,0:T(8,128)(2,1)}, bf16[256,256]{1,0:T(8,128)(2,1)}, bf16[32,256]{1,0:T(8,128)(2,1)}) custom-call(bf16[256,256]{1,0:T(8,128)(2,1)S(1)} %get-tuple-element.15.refs_0_, bf16[256,256]{1,0:T(8,128)(2,1)S(1)} %get-tuple-element.16.refs_1_, ...), custom_call_target="tpu_custom_call" | custom-call | tf_op jit(solution)/shard_map/pallas_call | solution.py:584
